TPU v7x, 256 devices: a whole 4x4x8 slice. The times are simulated.
256 devices in a mesh: batch: 32 (over y, x, core), rows: 8 (over z).
Axes of the slice: x: 4, y: 4, z: 8, core: 2. Of those that a mesh axis runs over, the one named last changes fastest.
Arguments:
- fine_level: bfloat16 [32, 64, 192, 384], P('batch', 'rows'), may hold values from -40 to 40
- middle_level: bfloat16 [32, 32, 96, 384], P('batch', 'rows'), may hold values from -40 to 40
- coarse_level: bfloat16 [32, 16, 48, 384], P('batch', 'rows'), may hold values from -40 to 40
- two_input_weights: float32 [2, 3, 2], replicated, may hold values from 0.5 to 2
- three_input_weights: float32 [2, 3], replicated, may hold values from 0.5 to 2
- depthwise: bfloat16 [2, 4, 3, 3, 384], replicated, may hold values from -2 to 2
- pointwise: bfloat16 [2, 4, 384, 384], replicated, may hold values from -0.3125 to 0.3125
- bn_gain: float32 [2, 4, 384], replicated, may hold values from 0.5 to 1.5
- bn_bias: float32 [2, 4, 384], replicated, may hold values from -3 to 3
Outputs:
- fine_result: bfloat16 [32, 64, 192, 384], P('batch', 'rows')
- middle_result: bfloat16 [32, 32, 96, 384], P('batch', 'rows')
- coarse_result: bfloat16 [32, 16, 48, 384], P('batch', 'rows')
All inputs are finite; a program needn't handle non-finite values.
Results may differ from a plain program's by a relative error of at most 0.025.
Values may be sent and summed in bfloat16 or wider, within the bound.
A program may use at most 64 MiB of HBM per device.

v0:
```python
import jax
import jax.numpy as jnp
from jax import lax
from jax.sharding import Mesh
from jax.sharding import PartitionSpec as P

LAYERS = 2
BATCH = ("batch_0", "batch_1", "batch_2")


def from_behind(block, axis, distance):
    devices = range(lax.axis_size(axis))
    route = [(i - distance, i) for i in devices if i - distance in devices]
    return lax.ppermute(block, axis, route)


def sent_to_all(value, axis):
    copies = jnp.broadcast_to(value, (lax.axis_size(axis), *value.shape))
    return lax.all_to_all(copies, axis, split_axis=0, concat_axis=0, tiled=True)


def over_copies(value, axis):
    return sent_to_all(value, axis).sum(axis=0)


def one_axis_at_a_time(value, axes):
    far, near = axes
    return over_copies(over_copies(value, near), far)


def packed_total(arrays, axis):
    vector, at, finished = (jnp.concatenate([a.reshape(-1) for a in arrays]), 0, [])
    total = one_axis_at_a_time(vector, axis)
    for a in arrays:
        finished.append(total[at : at + a.size].reshape(a.shape))
        at += a.size
    return tuple(finished)


def extended_2(block, sides, width):
    for axis, dim in sides:
        count = lax.axis_size(axis)
        forward = [(i, i + 1) for i in range(count - 1)]
        backward = [(target, source) for source, target in forward]
        low = lax.ppermute(
            lax.slice_in_dim(block, block.shape[dim] - width, None, axis=dim), axis, forward
        )
        high = lax.ppermute(lax.slice_in_dim(block, 0, width, axis=dim), axis, backward)
        block = jnp.concatenate([low, block, high], axis=dim)
    return block


def upsample(feature_maps):
    return jnp.repeat(jnp.repeat(feature_maps, 2, axis=1), 2, axis=2)


def reduce_resolution(feature_maps):
    beneath = from_behind(feature_maps[:, :1], "rows", -1)
    lowest = jnp.array(-jnp.inf, feature_maps.dtype)
    at_bottom = lax.axis_index("rows") == lax.axis_size("rows") - 1
    beneath = jnp.where(at_bottom, lowest, beneath)
    extended = jnp.concatenate([feature_maps, beneath], axis=1)
    padded = jnp.pad(extended, ((0, 0), (0, 0), (0, 1), (0, 0)), constant_values=lowest)
    return lax.reduce_window(padded, lowest, lax.max, (1, 3, 3, 1), (1, 2, 2, 1), "VALID")


def weighted_join_activate(inputs_list, weights):
    weight_sum = jnp.sum(weights) + 0.0001
    running = weights[0] * inputs_list[0].astype(jnp.float32)
    for position in range(1, len(inputs_list)):
        running = running + weights[position] * inputs_list[position].astype(jnp.float32)
    return jax.nn.silu(running / weight_sum).astype(jnp.bfloat16)


def separable(extended, kernel, projection):
    padded = jnp.pad(extended, ((0, 0), (0, 0), (1, 1), (0, 0)))
    height = extended.shape[1] - 2
    width = extended.shape[2]
    running = jnp.zeros((extended.shape[0], height, width, extended.shape[3]), jnp.float32)
    for row_tap in range(3):
        for col_tap in range(3):
            window = padded[:, row_tap : row_tap + height, col_tap : col_tap + width, :]
            running = running + window.astype(jnp.float32) * kernel[row_tap, col_tap].astype(
                jnp.float32
            )
    spatial = running.astype(jnp.bfloat16)
    projected = jnp.dot(
        spatial.reshape(-1, spatial.shape[-1]), projection, preferred_element_type=jnp.float32
    )
    return projected.reshape(spatial.shape)


def normalize(projected, gain, offset):
    count = float(
        projected.shape[0]
        * projected.shape[1]
        * projected.shape[2]
        * lax.axis_size(BATCH)
        * lax.axis_size("rows")
    )
    totals, squares = packed_total(
        (jnp.sum(projected, axis=(0, 1, 2)), jnp.sum(projected * projected, axis=(0, 1, 2))),
        (("batch_0", "batch_1"), ("batch_2", "rows")),
    )
    center = totals / count
    spread = squares / count - center * center
    centered = projected - center
    return (centered * lax.rsqrt(spread + 1e-05) * gain + offset).astype(jnp.bfloat16)


def node(activated, kernel, projection, gain, offset):
    extended = extended_2(activated, (("rows", 1),), 1)
    return normalize(separable(extended, kernel, projection), gain, offset)


def body(
    fine_level,
    middle_level,
    coarse_level,
    two_input_weights,
    three_input_weights,
    depthwise,
    pointwise,
    bn_gain,
    bn_bias,
):
    fine, middle_grid, coarse_grid = (fine_level, middle_level, coarse_level)
    for bidirectional_layer in range(LAYERS):

        def run_layer_pair(index, activated):
            return node(
                activated,
                depthwise[bidirectional_layer, index],
                pointwise[bidirectional_layer, index],
                bn_gain[bidirectional_layer, index],
                bn_bias[bidirectional_layer, index],
            )

        downward_middle = run_layer_pair(
            0,
            weighted_join_activate(
                [middle_grid, upsample(coarse_grid)], two_input_weights[bidirectional_layer, 0]
            ),
        )
        updated_fine = run_layer_pair(
            1,
            weighted_join_activate(
                [fine, upsample(downward_middle)], two_input_weights[bidirectional_layer, 1]
            ),
        )
        updated_middle = run_layer_pair(
            2,
            weighted_join_activate(
                [middle_grid, downward_middle, reduce_resolution(updated_fine)],
                three_input_weights[bidirectional_layer],
            ),
        )
        updated_coarse = run_layer_pair(
            3,
            weighted_join_activate(
                [coarse_grid, reduce_resolution(updated_middle)],
                two_input_weights[bidirectional_layer, 2],
            ),
        )
        fine, middle_grid, coarse_grid = (updated_fine, updated_middle, updated_coarse)
    return (fine, middle_grid, coarse_grid)


def solution(mesh):
    split = Mesh(
        mesh.devices.reshape(4, 4, 2, mesh.shape["rows"]), ("batch_0", "batch_1", "batch_2", "rows")
    )
    in_specs = (
        P(BATCH, "rows", None, None),
        P(BATCH, "rows", None, None),
        P(BATCH, "rows", None, None),
        P(),
        P(),
        P(),
        P(),
        P(),
        P(),
    )
    out_specs = (
        P(BATCH, "rows", None, None),
        P(BATCH, "rows", None, None),
        P(BATCH, "rows", None, None),
    )
    return jax.shard_map(body, mesh=split, in_specs=in_specs, out_specs=out_specs, check_vma=False)
```

profile of v0, /device:TPU:1, one launch (start us, length us, event | category | flops | bytes accessed | tf_op | source)
XLA Modules:
  0.0 369.2 jit_solution(15090444081342591841)
XLA Ops:
  7.6 4.4 %collective-permute-start = (bf16[1,1,96,384]{3,2,1,0:T(8,128)(2,1)S(1)}, bf16[1,1,96,384]{3,2,1,0:T(8,128)(2,1)S(1)}, u32[]{:S(2)}, u32[]{:S(2)}) collective-permute-start(bf16[1,1,96,384]{3,2,1,0:T(8,128)(2,1)S(1)} %get-tuple-element.125), channel_id=1, source_target_pairs={{0,1},{1,2},{2,3},{3,4},{4,5},{5,6},{6,7},{8,9},{9,10},{10,11},{11... | collective-permute-start | bytes 221192 | tf_op jit(solution)/shard_map/ppermute | solution.py:45
  19.2 17.1 %all_to_all.96 = f32[16,1,768]{2,1,0:T(1,128)S(1)} all-to-all(f32[16,1,768]{2,1,0:T(1,128)S(1)} %broadcast_in_dim.60), channel_id=1, replica_groups=mesh['batch_0'=4,'batch_1'=4,'batch_2'=2,'rows'=8] {'batch_2','rows'}, dimensions={0} | all-to-all | bytes 98304 | tf_op jit(solution)/shard_map/all_to_all | solution.py:19
  37.1 6.8 %all-to-all-start.1 = ((f32[16,1,768]{2,1,0:T(1,128)}), f32[16,1,768]{2,1,0:T(1,128)S(1)}, u32[]{:S(2)}, u32[]{:S(2)}) async-start(f32[16,1,768]{2,1,0:T(1,128)} %broadcast_in_dim.61), calls=%async_computation.1 | async-start | bytes 98304 | tf_op jit(solution)/shard_map/all_to_all | solution.py:19
  45.2 5.1 %all-to-all-done.1 = f32[16,1,768]{2,1,0:T(1,128)S(1)} async-done(((f32[16,1,768]{2,1,0:T(1,128)}), f32[16,1,768]{2,1,0:T(1,128)S(1)}, u32[]{:S(2)}, u32[]{:S(2)}) %all-to-all-start.1) | async-done | bytes 49184 | tf_op jit(solution)/shard_map/all_to_all | solution.py:19
  62.8 3.8 %collective-permute-done.3 = bf16[1,1,192,384]{3,2,1,0:T(8,128)(2,1)S(1)} collective-permute-done((bf16[1,1,192,384]{3,2,1,0:T(8,128)(2,1)S(1)}, bf16[1,1,192,384]{3,2,1,0:T(8,128)(2,1)S(1)}, u32[]{:S(2)}, u32[]{:S(2)}) %collective-permute-start.3) | collective-permute-done | bytes 147488 | tf_op jit(solution)/shard_map/ppermute | solution.py:48
  71.4 13.5 %all_to_all.97 = f32[16,1,768]{2,1,0:T(1,128)S(1)} all-to-all(f32[16,1,768]{2,1,0:T(1,128)S(1)} %broadcast_in_dim.64), channel_id=1, replica_groups=mesh['batch_0'=4,'batch_1'=4,'batch_2'=2,'rows'=8] {'batch_2','rows'}, dimensions={0} | all-to-all | bytes 98304 | tf_op jit(solution)/shard_map/all_to_all | solution.py:19
  85.6 3.5 all-to-all-start.3
  89.7 5.8 %all-to-all-done.3 = f32[16,1,768]{2,1,0:T(1,128)S(1)} async-done(((f32[16,1,768]{2,1,0:T(1,128)}), f32[16,1,768]{2,1,0:T(1,128)S(1)}, u32[]{:S(2)}, u32[]{:S(2)}) %all-to-all-start.3) | async-done | bytes 49184 | tf_op jit(solution)/shard_map/all_to_all | solution.py:19
  108.4 3.5 multiply_convert_fusion.4
  116.2 3.5 collective-permute-done.6
  121.7 15.1 %all_to_all.98 = f32[16,1,768]{2,1,0:T(1,128)S(1)} all-to-all(f32[16,1,768]{2,1,0:T(1,128)S(1)} %broadcast_in_dim.67), channel_id=1, replica_groups=mesh['batch_0'=4,'batch_1'=4,'batch_2'=2,'rows'=8] {'batch_2','rows'}, dimensions={0} | all-to-all | bytes 98304 | tf_op jit(solution)/shard_map/all_to_all | solution.py:19
  136.9 9.3 %all_to_all.99 = f32[16,1,768]{2,1,0:T(1,128)S(1)} all-to-all(f32[16,1,768]{2,1,0:T(1,128)S(1)} %broadcast_in_dim.68), channel_id=1, replica_groups=mesh['batch_0'=4,'batch_1'=4,'batch_2'=2,'rows'=8] {'batch_0','batch_1'}, dimensions={0} | all-to-all | bytes 98304 | tf_op jit(solution)/shard_map/all_to_all | solution.py:19
  163.7 15.3 %all_to_all.100 = f32[16,1,768]{2,1,0:T(1,128)S(1)} all-to-all(f32[16,1,768]{2,1,0:T(1,128)S(1)} %broadcast_in_dim.70), channel_id=1, replica_groups=mesh['batch_0'=4,'batch_1'=4,'batch_2'=2,'rows'=8] {'batch_2','rows'}, dimensions={0} | all-to-all | bytes 98304 | tf_op jit(solution)/shard_map/all_to_all | solution.py:19
  179.7 3.5 all-to-all-start.7
  183.9 5.7 %all-to-all-done.7 = f32[16,1,768]{2,1,0:T(1,128)S(1)} async-done(((f32[16,1,768]{2,1,0:T(1,128)}), f32[16,1,768]{2,1,0:T(1,128)S(1)}, u32[]{:S(2)}, u32[]{:S(2)}) %all-to-all-start.7) | async-done | bytes 49184 | tf_op jit(solution)/shard_map/all_to_all | solution.py:19
  200.4 3.7 %collective-permute-done.11 = bf16[1,1,96,384]{3,2,1,0:T(8,128)(2,1)S(1)} collective-permute-done((bf16[1,1,96,384]{3,2,1,0:T(8,128)(2,1)S(1)}, bf16[1,1,96,384]{3,2,1,0:T(8,128)(2,1)S(1)}, u32[]{:S(2)}, u32[]{:S(2)}) %collective-permute-start.11) | collective-permute-done | bytes 73760 | tf_op jit(solution)/shard_map/ppermute | solution.py:48
  206.9 13.2 %all_to_all.101 = f32[16,1,768]{2,1,0:T(1,128)S(1)} all-to-all(f32[16,1,768]{2,1,0:T(1,128)S(1)} %broadcast_in_dim.74), channel_id=1, replica_groups=mesh['batch_0'=4,'batch_1'=4,'batch_2'=2,'rows'=8] {'batch_2','rows'}, dimensions={0} | all-to-all | bytes 98304 | tf_op jit(solution)/shard_map/all_to_all | solution.py:19
  220.8 3.5 all-to-all-start.9
  224.9 5.8 %all-to-all-done.9 = f32[16,1,768]{2,1,0:T(1,128)S(1)} async-done(((f32[16,1,768]{2,1,0:T(1,128)}), f32[16,1,768]{2,1,0:T(1,128)S(1)}, u32[]{:S(2)}, u32[]{:S(2)}) %all-to-all-start.9) | async-done | bytes 49184 | tf_op jit(solution)/shard_map/all_to_all | solution.py:19
  234.9 4.1 %mul.1555 = f32[1,8,192,384]{3,2,1,0:T(8,128)} reshape(f32[8,96,2,384]{3,2,1,0:T(2,128)} %broadcast_in_dim.77) | data formatting | bytes 4718592 | tf_op jit(solution)/shard_map/mul | solution.py:71
  239.0 3.3 multiply_convert_fusion
  247.1 3.8 %collective-permute-done.13 = bf16[1,1,192,384]{3,2,1,0:T(8,128)(2,1)S(1)} collective-permute-done((bf16[1,1,192,384]{3,2,1,0:T(8,128)(2,1)S(1)}, bf16[1,1,192,384]{3,2,1,0:T(8,128)(2,1)S(1)}, u32[]{:S(2)}, u32[]{:S(2)}) %collective-permute-start.13) | collective-permute-done | bytes 147488 | tf_op jit(solution)/shard_map/ppermute | solution.py:48
  257.1 13.2 %all_to_all.102 = f32[16,1,768]{2,1,0:T(1,128)S(1)} all-to-all(f32[16,1,768]{2,1,0:T(1,128)S(1)} %broadcast_in_dim.78), channel_id=1, replica_groups=mesh['batch_0'=4,'batch_1'=4,'batch_2'=2,'rows'=8] {'batch_2','rows'}, dimensions={0} | all-to-all | bytes 98304 | tf_op jit(solution)/shard_map/all_to_all | solution.py:19
  271.0 3.5 all-to-all-start.11
  275.0 5.8 %all-to-all-done.11 = f32[16,1,768]{2,1,0:T(1,128)S(1)} async-done(((f32[16,1,768]{2,1,0:T(1,128)}), f32[16,1,768]{2,1,0:T(1,128)S(1)}, u32[]{:S(2)}, u32[]{:S(2)}) %all-to-all-start.11) | async-done | bytes 49184 | tf_op jit(solution)/shard_map/all_to_all | solution.py:19
  285.0 4.0 %collective-permute-done.14 = bf16[1,1,192,384]{3,2,1,0:T(8,128)(2,1)S(1)} collective-permute-done((bf16[1,1,192,384]{3,2,1,0:T(8,128)(2,1)S(1)}, bf16[1,1,192,384]{3,2,1,0:T(8,128)(2,1)S(1)}, u32[]{:S(2)}, u32[]{:S(2)}) %collective-permute-start.14) | collective-permute-done | bytes 147488 | tf_op jit(solution)/shard_map/ppermute | solution.py:14
  290.3 3.4 multiply_convert_fusion.2
  303.5 15.0 %all_to_all.103 = f32[16,1,768]{2,1,0:T(1,128)S(1)} all-to-all(f32[16,1,768]{2,1,0:T(1,128)S(1)} %broadcast_in_dim.80), channel_id=1, replica_groups=mesh['batch_0'=4,'batch_1'=4,'batch_2'=2,'rows'=8] {'batch_2','rows'}, dimensions={0} | all-to-all | bytes 98304 | tf_op jit(solution)/shard_map/all_to_all | solution.py:19
  318.6 9.3 %all_to_all.104 = f32[16,1,768]{2,1,0:T(1,128)S(1)} all-to-all(f32[16,1,768]{2,1,0:T(1,128)S(1)} %broadcast_in_dim.81), channel_id=1, replica_groups=mesh['batch_0'=4,'batch_1'=4,'batch_2'=2,'rows'=8] {'batch_0','batch_1'}, dimensions={0} | all-to-all | bytes 98304 | tf_op jit(solution)/shard_map/all_to_all | solution.py:19
  339.1 3.3 collective-permute-done.19
  343.8 15.3 %all_to_all.105 = f32[16,1,768]{2,1,0:T(1,128)S(1)} all-to-all(f32[16,1,768]{2,1,0:T(1,128)S(1)} %broadcast_in_dim.82), channel_id=1, replica_groups=mesh['batch_0'=4,'batch_1'=4,'batch_2'=2,'rows'=8] {'batch_2','rows'}, dimensions={0} | all-to-all | bytes 98304 | tf_op jit(solution)/shard_map/all_to_all | solution.py:19
  359.2 9.3 %all_to_all.106 = f32[16,1,768]{2,1,0:T(1,128)S(1)} all-to-all(f32[16,1,768]{2,1,0:T(1,128)S(1)} %broadcast_in_dim.83), channel_id=1, replica_groups=mesh['batch_0'=4,'batch_1'=4,'batch_2'=2,'rows'=8] {'batch_0','batch_1'}, dimensions={0} | all-to-all | bytes 98304 | tf_op jit(solution)/shard_map/all_to_all | solution.py:19
  (266 shorter events, 126.7 us)
Async XLA Ops:
  7.6 6.5 %collective-permute-start = (bf16[1,1,96,384]{3,2,1,0:T(8,128)(2,1)S(1)}, bf16[1,1,96,384]{3,2,1,0:T(8,128)(2,1)S(1)}, u32[]{:S(2)}, u32[]{:S(2)}) collective-permute-start(bf16[1,1,96,384]{3,2,1,0:T(8,128)(2,1)S(1)} %get-tuple-element.125), channel_id=1, source_target_pairs={{0,1},{1,2},{2,3},{3,4},{4,5},{5,6},{6,7},{8,9},{9,10},{10,11},{11... | collective-permute-start | bytes 221192 | tf_op jit(solution)/shard_map/ppermute | solution.py:45
  12.0 5.3 %collective-permute-start.1 = (bf16[1,1,96,384]{3,2,1,0:T(8,128)(2,1)S(1)}, bf16[1,1,96,384]{3,2,1,0:T(8,128)(2,1)S(1)}, u32[]{:S(2)}, u32[]{:S(2)}) collective-permute-start(bf16[1,1,96,384]{3,2,1,0:T(8,128)(2,1)S(1)} %get-tuple-element.126), channel_id=1, source_target_pairs={{1,0},{2,1},{3,2},{4,3},{5,4},{6,5},{7,6},{9,8},{10,9},{11,10},{12... | collective-permute-start | bytes 221192 | tf_op jit(solution)/shard_map/ppermute | solution.py:48
  37.1 13.2 %all-to-all-start.1 = ((f32[16,1,768]{2,1,0:T(1,128)}), f32[16,1,768]{2,1,0:T(1,128)S(1)}, u32[]{:S(2)}, u32[]{:S(2)}) async-start(f32[16,1,768]{2,1,0:T(1,128)} %broadcast_in_dim.61), calls=%async_computation.1 | async-start | bytes 98304 | tf_op jit(solution)/shard_map/all_to_all | solution.py:19
  58.1 4.7 %collective-permute-start.2 = (bf16[1,1,192,384]{3,2,1,0:T(8,128)(2,1)S(1)}, bf16[1,1,192,384]{3,2,1,0:T(8,128)(2,1)S(1)}, u32[]{:S(2)}, u32[]{:S(2)}) collective-permute-start(bf16[1,1,192,384]{3,2,1,0:T(8,128)(2,1)S(1)} %get-tuple-element.117), channel_id=1, source_target_pairs={{0,1},{1,2},{2,3},{3,4},{4,5},{5,6},{6,7},{8,9},{9,10},{10,11},{11... | collective-permute-start | bytes 442376 | tf_op jit(solution)/shard_map/ppermute | solution.py:45
  60.8 5.9 %collective-permute-start.3 = (bf16[1,1,192,384]{3,2,1,0:T(8,128)(2,1)S(1)}, bf16[1,1,192,384]{3,2,1,0:T(8,128)(2,1)S(1)}, u32[]{:S(2)}, u32[]{:S(2)}) collective-permute-start(bf16[1,1,192,384]{3,2,1,0:T(8,128)(2,1)S(1)} %get-tuple-element.118), channel_id=1, source_target_pairs={{1,0},{2,1},{3,2},{4,3},{5,4},{6,5},{7,6},{9,8},{10,9},{11,10},{12... | collective-permute-start | bytes 442376 | tf_op jit(solution)/shard_map/ppermute | solution.py:48
  85.6 9.9 %all-to-all-start.3 = ((f32[16,1,768]{2,1,0:T(1,128)}), f32[16,1,768]{2,1,0:T(1,128)S(1)}, u32[]{:S(2)}, u32[]{:S(2)}) async-start(f32[16,1,768]{2,1,0:T(1,128)} %broadcast_in_dim.65), calls=%async_computation.3 | async-start | bytes 98304 | tf_op jit(solution)/shard_map/all_to_all | solution.py:19
  97.9 6.2 %collective-permute-start.4 = (bf16[1,1,192,384]{3,2,1,0:T(8,128)(2,1)}, bf16[1,1,192,384]{3,2,1,0:T(8,128)(2,1)}, u32[]{:S(2)}, u32[]{:S(2)}) collective-permute-start(bf16[1,1,192,384]{3,2,1,0:T(8,128)(2,1)} %slice.1038), channel_id=1, source_target_pairs={{1,0},{2,1},{3,2},{4,3},{5,4},{6,5},{7,6},{9,8},{10,9},{11,10},{12... | collective-permute-start | bytes 442376 | tf_op jit(solution)/shard_map/ppermute | solution.py:14
  111.9 4.3 %collective-permute-start.5 = (bf16[1,1,96,384]{3,2,1,0:T(8,128)(2,1)S(1)}, bf16[1,1,96,384]{3,2,1,0:T(8,128)(2,1)S(1)}, u32[]{:S(2)}, u32[]{:S(2)}) collective-permute-start(bf16[1,1,96,384]{3,2,1,0:T(8,128)(2,1)S(1)} %get-tuple-element.123), channel_id=1, source_target_pairs={{0,1},{1,2},{2,3},{3,4},{4,5},{5,6},{6,7},{8,9},{9,10},{10,11},{11... | collective-permute-start | bytes 221192 | tf_op jit(solution)/shard_map/ppermute | solution.py:45
  114.6 5.1 %collective-permute-start.6 = (bf16[1,1,96,384]{3,2,1,0:T(8,128)(2,1)S(1)}, bf16[1,1,96,384]{3,2,1,0:T(8,128)(2,1)S(1)}, u32[]{:S(2)}, u32[]{:S(2)}) collective-permute-start(bf16[1,1,96,384]{3,2,1,0:T(8,128)(2,1)S(1)} %get-tuple-element.124), channel_id=1, source_target_pairs={{1,0},{2,1},{3,2},{4,3},{5,4},{6,5},{7,6},{9,8},{10,9},{11,10},{12... | collective-permute-start | bytes 221192 | tf_op jit(solution)/shard_map/ppermute | solution.py:48
  146.3 36.9 %copy-start.10 = (bf16[1,1,3,3,384]{4,1,3,2,0:T(2,128)(2,1)S(1)}, bf16[1,1,3,3,384]{4,1,3,2,0:T(2,128)(2,1)}, u32[]{:S(2)}) copy-start(bf16[1,1,3,3,384]{4,1,3,2,0:T(2,128)(2,1)} %get-tuple-element.132) | copy-start | bytes 20740
  146.3 36.9 %copy-start.11 = (bf16[1,1,3,3,384]{4,1,3,2,0:T(2,128)(2,1)S(1)}, bf16[1,1,3,3,384]{4,1,3,2,0:T(2,128)(2,1)}, u32[]{:S(2)}) copy-start(bf16[1,1,3,3,384]{4,1,3,2,0:T(2,128)(2,1)} %get-tuple-element.133) | copy-start | bytes 20740
  146.5 5.1 %collective-permute-start.7 = (bf16[1,1,96,384]{3,2,1,0:T(8,128)(2,1)S(1)}, bf16[1,1,96,384]{3,2,1,0:T(8,128)(2,1)S(1)}, u32[]{:S(2)}, u32[]{:S(2)}) collective-permute-start(bf16[1,1,96,384]{3,2,1,0:T(8,128)(2,1)S(1)} %slice.1056), channel_id=1, source_target_pairs={{1,0},{2,1},{3,2},{4,3},{5,4},{6,5},{7,6},{9,8},{10,9},{11,10},{12... | collective-permute-start | bytes 221192 | tf_op jit(solution)/shard_map/ppermute | solution.py:14
  154.9 4.0 %collective-permute-start.8 = (bf16[1,1,48,384]{3,2,1,0:T(8,128)(2,1)S(1)}, bf16[1,1,48,384]{3,2,1,0:T(8,128)(2,1)S(1)}, u32[]{:S(2)}, u32[]{:S(2)}) collective-permute-start(bf16[1,1,48,384]{3,2,1,0:T(8,128)(2,1)S(1)} %get-tuple-element.129), channel_id=1, source_target_pairs={{0,1},{1,2},{2,3},{3,4},{4,5},{5,6},{6,7},{8,9},{9,10},{10,11},{11... | collective-permute-start | bytes 110600 | tf_op jit(solution)/shard_map/ppermute | solution.py:45
  157.6 4.7 %collective-permute-start.9 = (bf16[1,1,48,384]{3,2,1,0:T(8,128)(2,1)S(1)}, bf16[1,1,48,384]{3,2,1,0:T(8,128)(2,1)S(1)}, u32[]{:S(2)}, u32[]{:S(2)}) collective-permute-start(bf16[1,1,48,384]{3,2,1,0:T(8,128)(2,1)S(1)} %get-tuple-element.130), channel_id=1, source_target_pairs={{1,0},{2,1},{3,2},{4,3},{5,4},{6,5},{7,6},{9,8},{10,9},{11,10},{12... | collective-permute-start | bytes 110600 | tf_op jit(solution)/shard_map/ppermute | solution.py:48
  158.9 35.4 %copy-start.16 = (f32[384]{0:T(512)S(1)}, f32[384]{0:T(512)}, u32[]{:S(2)}) copy-start(f32[384]{0:T(512)} %copy-done.15) | copy-start | bytes 4612
  159.0 35.3 %copy-start.18 = (f32[384]{0:T(512)S(1)}, f32[384]{0:T(512)}, u32[]{:S(2)}) copy-start(f32[384]{0:T(512)} %copy-done.17) | copy-start | bytes 4612
  179.7 9.9 %all-to-all-start.7 = ((f32[16,1,768]{2,1,0:T(1,128)}), f32[16,1,768]{2,1,0:T(1,128)S(1)}, u32[]{:S(2)}, u32[]{:S(2)}) async-start(f32[16,1,768]{2,1,0:T(1,128)} %broadcast_in_dim.71), calls=%async_computation.7 | async-start | bytes 98304 | tf_op jit(solution)/shard_map/all_to_all | solution.py:19
  196.3 4.0 %collective-permute-start.10 = (bf16[1,1,96,384]{3,2,1,0:T(8,128)(2,1)S(1)}, bf16[1,1,96,384]{3,2,1,0:T(8,128)(2,1)S(1)}, u32[]{:S(2)}, u32[]{:S(2)}) collective-permute-start(bf16[1,1,96,384]{3,2,1,0:T(8,128)(2,1)S(1)} %get-tuple-element.121), channel_id=1, source_target_pairs={{0,1},{1,2},{2,3},{3,4},{4,5},{5,6},{6,7},{8,9},{9,10},{10,11},{11... | collective-permute-start | bytes 221192 | tf_op jit(solution)/shard_map/ppermute | solution.py:45
  199.0 5.1 %collective-permute-start.11 = (bf16[1,1,96,384]{3,2,1,0:T(8,128)(2,1)S(1)}, bf16[1,1,96,384]{3,2,1,0:T(8,128)(2,1)S(1)}, u32[]{:S(2)}, u32[]{:S(2)}) collective-permute-start(bf16[1,1,96,384]{3,2,1,0:T(8,128)(2,1)S(1)} %get-tuple-element.122), channel_id=1, source_target_pairs={{1,0},{2,1},{3,2},{4,3},{5,4},{6,5},{7,6},{9,8},{10,9},{11,10},{12... | collective-permute-start | bytes 221192 | tf_op jit(solution)/shard_map/ppermute | solution.py:48
  220.8 9.9 %all-to-all-start.9 = ((f32[16,1,768]{2,1,0:T(1,128)}), f32[16,1,768]{2,1,0:T(1,128)S(1)}, u32[]{:S(2)}, u32[]{:S(2)}) async-start(f32[16,1,768]{2,1,0:T(1,128)} %broadcast_in_dim.75), calls=%async_computation.9 | async-start | bytes 98304 | tf_op jit(solution)/shard_map/all_to_all | solution.py:19
  242.4 4.7 %collective-permute-start.12 = (bf16[1,1,192,384]{3,2,1,0:T(8,128)(2,1)S(1)}, bf16[1,1,192,384]{3,2,1,0:T(8,128)(2,1)S(1)}, u32[]{:S(2)}, u32[]{:S(2)}) collective-permute-start(bf16[1,1,192,384]{3,2,1,0:T(8,128)(2,1)S(1)} %get-tuple-element.115), channel_id=1, source_target_pairs={{0,1},{1,2},{2,3},{3,4},{4,5},{5,6},{6,7},{8,9},{9,10},{10,11},{11... | collective-permute-start | bytes 442376 | tf_op jit(solution)/shard_map/ppermute | solution.py:45
  245.0 5.9 %collective-permute-start.13 = (bf16[1,1,192,384]{3,2,1,0:T(8,128)(2,1)S(1)}, bf16[1,1,192,384]{3,2,1,0:T(8,128)(2,1)S(1)}, u32[]{:S(2)}, u32[]{:S(2)}) collective-permute-start(bf16[1,1,192,384]{3,2,1,0:T(8,128)(2,1)S(1)} %get-tuple-element.116), channel_id=1, source_target_pairs={{1,0},{2,1},{3,2},{4,3},{5,4},{6,5},{7,6},{9,8},{10,9},{11,10},{12... | collective-permute-start | bytes 442376 | tf_op jit(solution)/shard_map/ppermute | solution.py:48
  271.0 9.9 %all-to-all-start.11 = ((f32[16,1,768]{2,1,0:T(1,128)}), f32[16,1,768]{2,1,0:T(1,128)S(1)}, u32[]{:S(2)}, u32[]{:S(2)}) async-start(f32[16,1,768]{2,1,0:T(1,128)} %broadcast_in_dim.79), calls=%async_computation.11 | async-start | bytes 98304 | tf_op jit(solution)/shard_map/all_to_all | solution.py:19
  283.1 5.9 %collective-permute-start.14 = (bf16[1,1,192,384]{3,2,1,0:T(8,128)(2,1)S(1)}, bf16[1,1,192,384]{3,2,1,0:T(8,128)(2,1)S(1)}, u32[]{:S(2)}, u32[]{:S(2)}) collective-permute-start(bf16[1,1,192,384]{3,2,1,0:T(8,128)(2,1)S(1)} %slice.1108), channel_id=1, source_target_pairs={{1,0},{2,1},{3,2},{4,3},{5,4},{6,5},{7,6},{9,8},{10,9},{11,10},{12... | collective-permute-start | bytes 442376 | tf_op jit(solution)/shard_map/ppermute | solution.py:14
  293.8 4.9 %collective-permute-start.15 = (bf16[1,1,96,384]{3,2,1,0:T(8,128)(2,1)S(1)}, bf16[1,1,96,384]{3,2,1,0:T(8,128)(2,1)S(1)}, u32[]{:S(2)}, u32[]{:S(2)}) collective-permute-start(bf16[1,1,96,384]{3,2,1,0:T(8,128)(2,1)S(1)} %get-tuple-element.119), channel_id=1, source_target_pairs={{0,1},{1,2},{2,3},{3,4},{4,5},{5,6},{6,7},{8,9},{9,10},{10,11},{11... | collective-permute-start | bytes 221192 | tf_op jit(solution)/shard_map/ppermute | solution.py:45
  296.4 5.1 %collective-permute-start.16 = (bf16[1,1,96,384]{3,2,1,0:T(8,128)(2,1)S(1)}, bf16[1,1,96,384]{3,2,1,0:T(8,128)(2,1)S(1)}, u32[]{:S(2)}, u32[]{:S(2)}) collective-permute-start(bf16[1,1,96,384]{3,2,1,0:T(8,128)(2,1)S(1)} %get-tuple-element.120), channel_id=1, source_target_pairs={{1,0},{2,1},{3,2},{4,3},{5,4},{6,5},{7,6},{9,8},{10,9},{11,10},{12... | collective-permute-start | bytes 221192 | tf_op jit(solution)/shard_map/ppermute | solution.py:48
  328.0 40.5 %copy-start.43 = (f32[384]{0:T(512)S(1)}, f32[384]{0:T(512)}, u32[]{:S(2)}) copy-start(f32[384]{0:T(512)} %get-tuple-element.27) | copy-start | bytes 4612
  328.0 40.5 %copy-start.44 = (f32[384]{0:T(512)S(1)}, f32[384]{0:T(512)}, u32[]{:S(2)}) copy-start(f32[384]{0:T(512)} %get-tuple-element.196) | copy-start | bytes 4612
  328.2 41.1 %copy-start.2 = (bf16[1,4,96,384]{3,2,1,0:T(8,128)(2,1)}, bf16[1,4,96,384]{3,2,1,0:T(8,128)(2,1)S(1)}, u32[]{:S(2)}) copy-start(bf16[1,4,96,384]{3,2,1,0:T(8,128)(2,1)S(1)} %add_convert_fusion.4) | copy-start | bytes 884740
  328.2 5.1 %collective-permute-start.17 = (bf16[1,1,96,384]{3,2,1,0:T(8,128)(2,1)S(1)}, bf16[1,1,96,384]{3,2,1,0:T(8,128)(2,1)S(1)}, u32[]{:S(2)}, u32[]{:S(2)}) collective-permute-start(bf16[1,1,96,384]{3,2,1,0:T(8,128)(2,1)S(1)} %slice.1126), channel_id=1, source_target_pairs={{1,0},{2,1},{3,2},{4,3},{5,4},{6,5},{7,6},{9,8},{10,9},{11,10},{12... | collective-permute-start | bytes 221192 | tf_op jit(solution)/shard_map/ppermute | solution.py:14
  335.0 4.0 %collective-permute-start.18 = (bf16[1,1,48,384]{3,2,1,0:T(8,128)(2,1)S(1)}, bf16[1,1,48,384]{3,2,1,0:T(8,128)(2,1)S(1)}, u32[]{:S(2)}, u32[]{:S(2)}) collective-permute-start(bf16[1,1,48,384]{3,2,1,0:T(8,128)(2,1)S(1)} %get-tuple-element.127), channel_id=1, source_target_pairs={{0,1},{1,2},{2,3},{3,4},{4,5},{5,6},{6,7},{8,9},{9,10},{10,11},{11... | collective-permute-start | bytes 110600 | tf_op jit(solution)/shard_map/ppermute | solution.py:45
  337.7 4.7 %collective-permute-start.19 = (bf16[1,1,48,384]{3,2,1,0:T(8,128)(2,1)S(1)}, bf16[1,1,48,384]{3,2,1,0:T(8,128)(2,1)S(1)}, u32[]{:S(2)}, u32[]{:S(2)}) collective-permute-start(bf16[1,1,48,384]{3,2,1,0:T(8,128)(2,1)S(1)} %get-tuple-element.128), channel_id=1, source_target_pairs={{1,0},{2,1},{3,2},{4,3},{5,4},{6,5},{7,6},{9,8},{10,9},{11,10},{12... | collective-permute-start | bytes 110600 | tf_op jit(solution)/shard_map/ppermute | solution.py:48
  (40 other events, 669.7 us)
where the time goes:
time: 372 us; the launch traced here: 369 us
  blocking collectives  146 us (39%)
  waiting for transfers between devices  68.5 us (18%)
  starting transfers between devices  59.5 us (16%)
  other arithmetic  47.8 us (13%)
  local copies, waits for them, and re-layouts  26.8 us (7%)
  matrix products  13.7 us (4%)
  between operations  7.17 us (2%)
    all_to_all x11, blocking collectives, sent_to_all(): return lax.all_to_all(copies, axis, split_axis=0, concat_axis=0, tiled=True)  146 us
    all_to_all x5, waiting for transfers between devices, sent_to_all(): return lax.all_to_all(copies, axis, split_axis=0, concat_axis=0, tiled=True)  28.1 us
    ppermute x8, waiting for transfers between devices, extended_2(): lax.ppermute(lax.slice_in_dim(block, 0, width, axis=dim), axis, backward)  27.6 us
    ppermute x8, starting transfers between devices, extended_2(): lax.ppermute(lax.slice_in_dim(block, block.shape[dim] - width, None, axis...  22.9 us
    all_to_all x5, starting transfers between devices, sent_to_all(): return lax.all_to_all(copies, axis, split_axis=0, concat_axis=0, tiled=True)  20.8 us
    convert_element_type x8, other arithmetic, weighted_join_activate(): return jax.nn.silu(running / weight_sum).astype(jnp.bfloat16)  17 us
    dot_general x8, matrix products, separable(): jnp.dot(spatial.reshape(-1, spatial.shape[-1]), projection, preferred_ele...  13.7 us
    ppermute x4, waiting for transfers between devices, from_behind(): return lax.ppermute(block, axis, route)  11.6 us
  transfers between devices with their start and end apart: 25, of which 19 were waited for; matrix products, arithmetic and copies ran while one was open for 2% of the time, Pallas kernels for 0%

commit v1 on v0

v1 whole, which is shorter than its diff:
```python
import functools

import jax
import jax.numpy as jnp
from jax import lax
from jax.experimental import pallas as pl
from jax.experimental.pallas import tpu as pltpu
from jax.sharding import Mesh
from jax.sharding import PartitionSpec as P

LAYERS = 2
BATCH = ("batch_0", "batch_1", "batch_2")
MESH_ID = pl.DeviceIdType.MESH
HUB = 1
C = 384
K = 48
LOW = -1e30
EPS = 1e-05
F32 = jnp.float32
BF16 = jnp.bfloat16


def ring_distance(d, n):
    return min(d, n - d)


Z_OFFSETS = sorted(range(1, 8), key=lambda d: -ring_distance(d, 8))
XY_OFFSETS = sorted(
    [(a, b) for a in range(4) for b in range(4) if (a, b) != (0, 0)],
    key=lambda o: -(ring_distance(o[0], 4) + ring_distance(o[1], 4)),
)


def tiles(x):
    return x.reshape(x.shape[0] // 8, 8, x.shape[1])


def flat(x):
    return x.reshape(x.shape[0] * x.shape[1], x.shape[2])


def shifted_down(x):
    rolled = pltpu.roll(x, 1, axis=0)
    return jnp.where(lax.broadcasted_iota(jnp.int32, x.shape, 0) == 0, 0.0, rolled)


def shifted_up(x, fill):
    rolled = pltpu.roll(x, x.shape[0] - 1, axis=0)
    at_end = lax.broadcasted_iota(jnp.int32, x.shape, 0) == x.shape[0] - 1
    return jnp.where(at_end, fill, rolled)


def silu_of_double(h):
    return h + h * jnp.tanh(h)


def wait_bytes(ref, sem):
    pltpu.make_async_copy(ref, ref, sem).wait()


def kernel(
    counts,
    fine_hbm,
    mid_hbm,
    top_hbm,
    w2,
    w3,
    dw_hbm,
    pw_hbm,
    gain_hbm,
    bias_hbm,
    fine_out,
    mid_out,
    top_out,
    fine_nat,
    mid_nat,
    top_nat,
    dw_in,
    pw,
    gain,
    bias,
    dwb,
    perm_f,
    perm_m,
    back_f,
    back_m,
    base_f,
    act_f,
    mid_in,
    base_m,
    act_m,
    top_in,
    base_t,
    act_t,
    lifted,
    raw_m,
    raw_f,
    raw_t,
    col_f,
    col_m,
    pool_m,
    pool_t,
    spat,
    norm,
    halo_m,
    send_m,
    halo_p,
    send_p,
    halo_f,
    send_f,
    halo_q,
    send_q,
    halo_t,
    send_t,
    halo_c,
    send_c,
    ring,
    plane,
    fine_res,
    mid_res,
    top_res,
    in_sem,
    out_sem,
    ring_s,
    ring_r,
    plane_s,
    plane_r,
    halo_s,
    halo_r,
):
    y, x = lax.axis_index("batch_0"), lax.axis_index("batch_1")
    core, z = lax.axis_index("batch_2"), lax.axis_index("rows")
    in_ring = core * 8 + z
    in_plane = y * 4 + x
    is_hub = core == HUB
    has_above, has_below = z > 0, z < 7

    barrier = pltpu.get_barrier_semaphore()

    def greet(**device):
        pl.semaphore_signal(barrier, inc=1, device_id=device, device_id_type=MESH_ID)

    for d in range(8):
        for c in range(2):
            if d:
                greet(batch_2=lax.rem(core + c, 2), rows=lax.rem(z + d, 8))
    for a in range(4):
        for b in range(4):
            for c in range(2):
                if (a, b, c) != (0, 0, 0):
                    greet(
                        batch_0=lax.rem(y + a, 4),
                        batch_1=lax.rem(x + b, 4),
                        batch_2=lax.rem(core + c, 2),
                    )

    loads = {
        "top": pltpu.make_async_copy(top_hbm.at[0], top_nat.at[pl.ds(1, 2)], in_sem.at[0]),
        "mid": pltpu.make_async_copy(mid_hbm.at[0], mid_nat.at[pl.ds(1, 4)], in_sem.at[1]),
        "dw": pltpu.make_async_copy(dw_hbm, dw_in, in_sem.at[2]),
        "fine": pltpu.make_async_copy(fine_hbm.at[0], fine_nat.at[pl.ds(1, 8)], in_sem.at[3]),
        "pw": pltpu.make_async_copy(pw_hbm, pw, in_sem.at[4]),
        "gain": pltpu.make_async_copy(gain_hbm, gain, in_sem.at[5]),
        "bias": pltpu.make_async_copy(bias_hbm, bias, in_sem.at[6]),
    }
    for load in loads.values():
        load.start()

    def permutation(ref, back, parts):
        n = parts * K
        row = lax.broadcasted_iota(jnp.int32, (n, n), 0)
        col = lax.broadcasted_iota(jnp.int32, (n, n), 1)
        ref[...] = jnp.where(lax.rem(row, K) * parts + lax.div(row, K) == col, 1.0, 0.0).astype(BF16)
        back[...] = jnp.where(lax.rem(col, K) * parts + lax.div(col, K) == row, 1.0, 0.0).astype(
            BF16
        )

    permutation(perm_m, back_m, 2)
    permutation(perm_f, back_f, 4)

    def zeroed(ref):
        ref[...] = jnp.zeros(ref.shape, ref.dtype)

    @pl.when(z == 0)
    def _():
        for ref in (fine_nat.at[0], mid_nat.at[0], top_nat.at[0]):
            zeroed(ref)
        for l in range(LAYERS):
            for ref in (halo_m.at[l, 0], halo_p.at[l, 0], halo_q.at[l, 0]):
                zeroed(ref)
        for ref in (halo_f.at[0], halo_t.at[0], halo_c.at[0]):
            zeroed(ref)
        for node in range(8):
            zeroed(norm.at[node, 3])

    @pl.when(z == 7)
    def _():
        for ref in (fine_nat.at[9], mid_nat.at[5], top_nat.at[3]):
            zeroed(ref)
        for l in range(LAYERS):
            zeroed(halo_m.at[l, 1])
            for s in (1, 2):
                for ref in (halo_p.at[l, s], halo_q.at[l, s]):
                    ref[...] = jnp.full(ref.shape, LOW, BF16)
        for ref in (halo_f.at[1], halo_t.at[1], halo_c.at[1]):
            zeroed(ref)
        for node in range(8):
            zeroed(norm.at[node, 4])

    loads["dw"].wait()
    for l in range(LAYERS):
        for n in range(4):
            for i in range(3):
                taps = dw_in[l, n, i].astype(F32)
                for j in range(3):
                    dwb[l * 4 + n, 3 * i + j] = jnp.broadcast_to(taps[j : j + 1], (8, C))

    pl.semaphore_wait(barrier, 14 + 31)

    above = {"rows": jnp.maximum(z - 1, 0)}
    below = {"rows": jnp.minimum(z + 1, 7)}

    def to_above(src, dst, slot):
        return pltpu.make_async_remote_copy(
            src, dst, halo_s.at[slot], halo_r.at[slot], device_id=above, device_id_type=MESH_ID
        )

    def to_below(src, dst, slot):
        return pltpu.make_async_remote_copy(
            src, dst, halo_s.at[slot], halo_r.at[slot], device_id=below, device_id_type=MESH_ID
        )

    sends_up, sends_down = [], []

    def send(up, down):
        @pl.when(has_above)
        def _():
            for one in up:
                to_above(*one).start()

        @pl.when(has_below)
        def _():
            for one in down:
                to_below(*one).start()

        sends_up.extend(up)
        sends_down.extend(down)

    def receive(from_below, from_above):
        @pl.when(has_below)
        def _():
            for _, dst, slot in from_below:
                wait_bytes(dst, halo_r.at[slot])

        @pl.when(has_above)
        def _():
            for _, dst, slot in from_above:
                wait_bytes(dst, halo_r.at[slot])

    loads["top"].wait()
    loads["mid"].wait()
    first_up = [
        (mid_nat.at[1], mid_nat.at[5], 0),
        (top_nat.at[1], top_nat.at[3], 1),
    ]
    first_down = [
        (mid_nat.at[4], mid_nat.at[0], 2),
        (top_nat.at[2], top_nat.at[0], 3),
    ]
    send(first_up, first_down)
    loads["fine"].wait()
    fine_up = [(fine_nat.at[1], fine_nat.at[9], 4)]
    fine_down = [(fine_nat.at[8], fine_nat.at[0], 5)]
    send(fine_up, fine_down)

    def halves(weights):
        spread = [jnp.full((8, C), 1.0, F32) * w for w in weights]
        acc = spread[0]
        for one in spread[1:]:
            acc = acc + one
        acc = acc + 0.0001
        return [0.5 * one / acc for one in spread]

    def two(l, n):
        return halves([w2[l, n, 0], w2[l, n, 1]])

    def three(l):
        return halves([w3[l, 0], w3[l, 1], w3[l, 2]])

    def convolve(act, raw, index, height, planes, step_rows):
        lanes = planes * K

        def step(s, carry):
            total, squares = carry
            for dr in range(step_rows):
                r = s * step_rows + dr
                for c in range(3):
                    cs = pl.ds(c * 128, 128)
                    taps = [dwb[index, t, :, cs] for t in range(9)]
                    sums = []
                    for q in range(planes):
                        rows = [tiles(act[r + i, q, :, cs]) for i in range(3)]
                        sums.append(
                            [
                                flat(
                                    rows[0] * taps[j] + rows[1] * taps[3 + j] + rows[2] * taps[6 + j]
                                )
                                for j in range(3)
                            ]
                        )
                    for q in range(planes):
                        left = sums[q - 1][0] if q else shifted_down(sums[planes - 1][0])
                        right = sums[q + 1][2] if q + 1 < planes else shifted_up(sums[0][2], 0.0)
                        spat[pl.ds(dr * lanes + q * K, K), cs] = (left + sums[q][1] + right).astype(
                            BF16
                        )
            out = jnp.dot(
                spat[pl.ds(0, step_rows * lanes), :],
                pw[index // 4, index % 4],
                preferred_element_type=F32,
            )
            for dr in range(step_rows):
                for q in range(planes):
                    at = dr * lanes + q * K
                    raw[s * step_rows + dr, q] = out[at : at + K]
            out = tiles(out)
            return total + jnp.sum(out, axis=0), squares + jnp.sum(out * out, axis=0)

        start = (jnp.zeros((8, C), F32), jnp.zeros((8, C), F32))
        return lax.fori_loop(0, height // step_rows, step, start)

    def reduce_start(index, stats, local_count):
        total, squares = stats
        total = jnp.sum(total, axis=0, keepdims=True)
        squares = jnp.sum(squares, axis=0, keepdims=True)
        for c in range(3):
            ring[index, in_ring, c : c + 1, :] = total[:, c * 128 : (c + 1) * 128]
            ring[index, in_ring, 3 + c : 4 + c, :] = squares[:, c * 128 : (c + 1) * 128]
        norm[index, 2] = jnp.broadcast_to(total * (1.0 / local_count), (8, C))

        def to_hub(**device):
            pltpu.make_async_remote_copy(
                ring.at[index, in_ring],
                ring.at[index, in_ring],
                ring_s.at[index],
                ring_r.at[index],
                device_id=device,
                device_id_type=MESH_ID,
            ).start()

        @pl.when(jnp.logical_not(is_hub))
        def _():
            for d in Z_OFFSETS + [0]:
                to_hub(batch_2=HUB, rows=lax.rem(z + d, 8))

        @pl.when(is_hub)
        def _():
            for d in Z_OFFSETS:
                to_hub(rows=lax.rem(z + d, 8))
            wait_bytes(ring.at[index, pl.ds(0, 15)], ring_r.at[index])
            acc = ring[index, 0]
            for k in range(1, 16):
                acc = acc + ring[index, k]
            plane[index * 16 + in_plane] = acc

            def to_plane(**device):
                pltpu.make_async_remote_copy(
                    plane.at[index * 16 + in_plane],
                    plane.at[index * 16 + in_plane],
                    plane_s.at[index],
                    plane_r.at[index],
                    device_id=device,
                    device_id_type=MESH_ID,
                ).start()

            for a, b in XY_OFFSETS:
                at = {"batch_0": lax.rem(y + a, 4), "batch_1": lax.rem(x + b, 4)}
                to_plane(**at, batch_2=1 - HUB)
                to_plane(**at)
            to_plane(batch_2=1 - HUB)

    def reduce_end(index, count):
        @pl.when(is_hub)
        def _():
            wait_bytes(plane.at[pl.ds(index * 16, 15)], plane_r.at[index])

        @pl.when(jnp.logical_not(is_hub))
        def _():
            wait_bytes(plane.at[pl.ds(index * 16, 16)], plane_r.at[index])

        acc = plane[index * 16]
        for k in range(1, 16):
            acc = acc + plane[index * 16 + k]
        acc = acc * (1.0 / count)
        l, n = index // 4, index % 4
        for c in range(3):
            cs = pl.ds(c * 128, 128)
            center = acc[c : c + 1]
            spread = acc[3 + c : 4 + c] - center * center
            scale = gain[l, n : n + 1, cs] * lax.rsqrt(spread + EPS)
            shift = bias[l, n : n + 1, cs] - center * scale
            norm[index, 0, :, cs] = jnp.broadcast_to(scale, (8, 128))
            norm[index, 1, :, cs] = jnp.broadcast_to(shift, (8, 128))

    def centred(value, index):
        return flat(tiles(value) - norm[index, 2]).astype(BF16)

    def mean_up(index):
        return (norm.at[index, 2], norm.at[index, 4], 8 + 2 * index)

    def mean_down(index):
        return (norm.at[index, 2], norm.at[index, 3], 9 + 2 * index)

    def scale_shift(index, weight):
        scale, shift = norm[index, 0], norm[index, 1]
        if weight is not None:
            scale, shift = scale * weight, shift * weight
        shift_above = norm[index, 3] * scale + shift
        shift_below = norm[index, 4] * scale + shift
        return scale, shift, shift_above, shift_below

    def affine(value, scale, shift):
        return flat(tiles(value.astype(F32)) * scale + shift)

    def masked_edges(act, last):
        @pl.when(z == 0)
        def _():
            zeroed(act.at[0])

        @pl.when(z == 7)
        def _():
            zeroed(act.at[last])

    def each(n, fn):
        def step(i, _):
            fn(i)
            return 0

        lax.fori_loop(0, n, step, 0)

    def column_pool(load, planes):
        out = []
        for p in range(max(planes // 2, 1)):
            x0, x1 = load(2 * p), load(2 * p + 1)
            x2 = load(2 * p + 2) if 2 * p + 2 < planes else shifted_up(load(0), LOW)
            out.append(jnp.maximum(jnp.maximum(x0, x1), x2))
        return out

    mid_pair = range(2)

    for l in range(LAYERS):
        i0, i1, i2, i3 = (4 * l + n for n in range(4))
        mids = raw_m.at[2 * l]
        fines = raw_f.at[l]
        nexts = raw_m.at[2 * l + 1]
        tops = raw_t.at[l]

        own, up = two(l, 0)
        if l == 0:
            receive(first_up, first_down)

            def place_mid(e):
                out = jnp.dot(perm_m[...], mid_nat[e], preferred_element_type=F32)
                for p in mid_pair:
                    mid_in[e, p] = out[p * K : (p + 1) * K]

            each(6, place_mid)
            for e in range(4):
                top_in[e] = top_nat[e].astype(F32)
            loads["pw"].wait()
            loads["gain"].wait()
            loads["bias"].wait()
        else:
            scale, shift, shift_above, shift_below = scale_shift(3, None)
            for e in range(4):
                if e == 0:
                    top_in[e] = affine(halo_c[0], scale, shift_above)
                elif e == 3:
                    top_in[e] = affine(halo_c[1], scale, shift_below)
                else:
                    top_in[e] = affine(raw_t[0, e - 1, 0], scale, shift)

        def join_0(e):
            t = tiles(top_in[lax.div(e + 1, 2)]) * up
            for p in mid_pair:
                act_m[e, p] = flat(silu_of_double(tiles(mid_in[e, p]) * own + t))

        each(6, join_0)
        masked_edges(act_m, 5)
        stats = convolve(act_m, mids, i0, 4, 2, 2)
        reduce_start(i0, stats, 4 * 96)
        for p in mid_pair:
            send_m[l, 0, p] = centred(mids[0, p], i0)
            send_m[l, 1, p] = centred(mids[3, p], i0)
        up_0 = [(send_m.at[l, 0], halo_m.at[l, 1], 24 + 2 * l), mean_up(i0)]
        down_0 = [(send_m.at[l, 1], halo_m.at[l, 0], 25 + 2 * l), mean_down(i0)]
        send(up_0, down_0)

        own, up = two(l, 1)
        if l == 0:
            receive(fine_up, fine_down)

            def place_fine(e):
                out = jnp.dot(perm_f[...], fine_nat[e], preferred_element_type=F32)
                for q in range(4):
                    base_f[e, q] = flat(tiles(out[q * K : (q + 1) * K]) * own)

            each(10, place_fine)
        else:
            scale, shift, shift_above, shift_below = scale_shift(1, own)

            def place_fine(e):
                for q in range(4):
                    base_f[e + 1, q] = affine(raw_f[0, e, q], scale, shift)

            each(8, place_fine)
            for q in range(4):
                base_f[0, q] = affine(halo_f[0, q], scale, shift_above)
                base_f[9, q] = affine(halo_f[1, q], scale, shift_below)

        receive(up_0, down_0)
        reduce_end(i0, counts[1])

        scale, shift, shift_above, shift_below = scale_shift(i0, up)
        for p in mid_pair:
            lifted[0, p] = affine(halo_m[l, 0, p], scale, shift_above)
            lifted[5, p] = affine(halo_m[l, 1, p], scale, shift_below)

        def lift(e):
            for p in mid_pair:
                lifted[e + 1, p] = affine(mids[e, p], scale, shift)

        each(4, lift)

        def join_1(e):
            m = lax.div(e + 1, 2)
            for p in mid_pair:
                t = lifted[m, p]
                for q in (2 * p, 2 * p + 1):
                    act_f[e, q] = silu_of_double(base_f[e, q] + t)

        each(10, join_1)
        masked_edges(act_f, 9)
        stats = convolve(act_f, fines, i1, 8, 4, 1)
        reduce_start(i1, stats, 8 * 192)

        def pool_columns(r):
            for p, out in enumerate(column_pool(lambda q: fines[r, q], 4)):
                col_f[r, p] = out

        each(8, pool_columns)
        for p in mid_pair:
            first = jnp.maximum(jnp.maximum(col_f[0, p], col_f[1, p]), col_f[2, p])
            pool_m[1, p] = first
            send_p[l, 0, p] = centred(col_f[0, p], i1)
            send_p[l, 1, p] = centred(first, i1)
            send_p[l, 2, p] = centred(jnp.maximum(col_f[6, p], col_f[7, p]), i1)
        up_1 = [(send_p.at[l, pl.ds(0, 2)], halo_p.at[l, pl.ds(1, 2)], 28 + 2 * l), mean_up(i1)]
        down_1 = [(send_p.at[l, 2], halo_p.at[l, 0], 29 + 2 * l), mean_down(i1)]
        send(up_1, down_1)
        if l == 0:
            for q in range(4):
                send_f[0, q] = centred(fines[0, q], i1)
                send_f[1, q] = centred(fines[7, q], i1)
            up_f = [(send_f.at[0], halo_f.at[1], 32)]
            down_f = [(send_f.at[1], halo_f.at[0], 33)]
            send(up_f, down_f)

        w_mid, w_down, w_pool = three(l)
        scale, shift, shift_above, shift_below = scale_shift(i0, w_down)

        def known(e, value, one_shift):
            for p in mid_pair:
                base_m[e, p] = flat(
                    tiles(mid_in[e, p]) * w_mid + tiles(value(p).astype(F32)) * scale + one_shift
                )

        known(0, lambda p: halo_m[l, 0, p], shift_above)
        known(5, lambda p: halo_m[l, 1, p], shift_below)
        each(4, lambda e: known(e + 1, lambda p: mids[e, p], shift))
        w_top, w_up = two(l, 2)
        for e in range(4):
            base_t[e] = flat(tiles(top_in[e]) * w_top)
        for i in (1, 2):
            for p in mid_pair:
                pool_m[i + 1, p] = jnp.maximum(
                    jnp.maximum(col_f[2 * i, p], col_f[2 * i + 1, p]), col_f[2 * i + 2, p]
                )
        receive(up_1, down_1)
        mean_above, mean_below = norm[i1, 3], norm[i1, 4]
        for p in mid_pair:
            pool_m[0, p] = jnp.maximum(
                flat(tiles(halo_p[l, 0, p].astype(F32)) + mean_above), col_f[0, p]
            )
            pool_m[4, p] = jnp.maximum(
                jnp.maximum(col_f[6, p], col_f[7, p]),
                flat(tiles(halo_p[l, 1, p].astype(F32)) + mean_below),
            )
            pool_m[5, p] = flat(tiles(halo_p[l, 2, p].astype(F32)) + mean_below)
        reduce_end(i1, counts[0])

        scale, shift, _, _ = scale_shift(i1, w_pool)

        def join_2(e):
            for p in mid_pair:
                act_m[e, p] = flat(
                    silu_of_double(tiles(base_m[e, p]) + (tiles(pool_m[e, p]) * scale + shift))
                )

        each(6, join_2)
        masked_edges(act_m, 5)
        stats = convolve(act_m, nexts, i2, 4, 2, 2)
        reduce_start(i2, stats, 4 * 96)
        for r in range(4):
            col_m[r] = column_pool(lambda q: nexts[r, q], 2)[0]
        first = jnp.maximum(jnp.maximum(col_m[0], col_m[1]), col_m[2])
        pool_t[1] = first
        send_q[l, 0] = centred(col_m[0], i2)
        send_q[l, 1] = centred(first, i2)
        send_q[l, 2] = centred(jnp.maximum(col_m[2], col_m[3]), i2)
        up_2 = [(send_q.at[l, pl.ds(0, 2)], halo_q.at[l, pl.ds(1, 2)], 34 + 2 * l), mean_up(i2)]
        down_2 = [(send_q.at[l, 2], halo_q.at[l, 0], 35 + 2 * l), mean_down(i2)]
        send(up_2, down_2)
        if l == 0:
            for p in mid_pair:
                send_t[0, p] = centred(nexts[0, p], i2)
                send_t[1, p] = centred(nexts[3, p], i2)
            up_t = [(send_t.at[0], halo_t.at[1], 38)]
            down_t = [(send_t.at[1], halo_t.at[0], 39)]
            send(up_t, down_t)
            receive(up_f, down_f)
        else:
            scale, shift, _, _ = scale_shift(i1, None)

            def finish_fine(r):
                for q in range(4):
                    spat[pl.ds(q * K, K), :] = affine(fines[r, q], scale, shift).astype(BF16)
                fine_res[r] = jnp.dot(
                    back_f[...], spat[pl.ds(0, 4 * K), :], preferred_element_type=F32
                ).astype(BF16)

            each(8, finish_fine)
            fine_store = pltpu.make_async_copy(fine_res, fine_out.at[0], out_sem.at[0])
            fine_store.start()
        receive(up_2, down_2)
        mean_above, mean_below = norm[i2, 3], norm[i2, 4]
        pool_t[0] = jnp.maximum(flat(tiles(halo_q[l, 0].astype(F32)) + mean_above), col_m[0])
        pool_t[2] = jnp.maximum(
            jnp.maximum(col_m[2], col_m[3]), flat(tiles(halo_q[l, 1].astype(F32)) + mean_below)
        )
        pool_t[3] = flat(tiles(halo_q[l, 2].astype(F32)) + mean_below)
        reduce_end(i2, counts[1])

        scale, shift, _, _ = scale_shift(i2, w_up)
        for e in range(4):
            act_t[e, 0] = flat(
                silu_of_double(tiles(base_t[e]) + (tiles(pool_t[e]) * scale + shift))
            )
        masked_edges(act_t, 3)
        stats = convolve(act_t, tops, i3, 2, 1, 2)
        reduce_start(i3, stats, 2 * 48)
        scale, shift, shift_above, shift_below = scale_shift(i2, None)
        if l == 0:
            send_c[0] = centred(tops[0, 0], i3)
            send_c[1] = centred(tops[1, 0], i3)
            up_3 = [(send_c.at[0], halo_c.at[1], 40), mean_up(i3)]
            down_3 = [(send_c.at[1], halo_c.at[0], 41), mean_down(i3)]
            send(up_3, down_3)
            receive(up_t, down_t)
            for p in mid_pair:
                mid_in[0, p] = affine(halo_t[0, p], scale, shift_above)
                mid_in[5, p] = affine(halo_t[1, p], scale, shift_below)

            def normalize_mid(e):
                for p in mid_pair:
                    mid_in[e + 1, p] = affine(nexts[e, p], scale, shift)

            each(4, normalize_mid)
            receive(up_3, down_3)
            reduce_end(i3, counts[2])
        else:

            def finish_mid(r):
                for p in mid_pair:
                    spat[pl.ds(p * K, K), :] = affine(nexts[r, p], scale, shift).astype(BF16)
                mid_res[r] = jnp.dot(
                    back_m[...], spat[pl.ds(0, 2 * K), :], preferred_element_type=F32
                ).astype(BF16)

            each(4, finish_mid)
            mid_store = pltpu.make_async_copy(mid_res, mid_out.at[0], out_sem.at[1])
            mid_store.start()
            reduce_end(i3, counts[2])
            scale, shift, _, _ = scale_shift(i3, None)
            for e in range(2):
                top_res[e] = affine(tops[e, 0], scale, shift).astype(BF16)
            top_store = pltpu.make_async_copy(top_res, top_out.at[0], out_sem.at[2])
            top_store.start()

    @pl.when(has_above)
    def _():
        for src, _, slot in sends_up:
            wait_bytes(src, halo_s.at[slot])

    @pl.when(has_below)
    def _():
        for src, _, slot in sends_down:
            wait_bytes(src, halo_s.at[slot])

    @pl.when(jnp.logical_not(is_hub))
    def _():
        for index in range(8):
            wait_bytes(ring.at[index, pl.ds(0, 8)], ring_s.at[index])

    @pl.when(is_hub)
    def _():
        for index in range(8):
            wait_bytes(ring.at[index, pl.ds(0, 7)], ring_s.at[index])
            wait_bytes(plane.at[pl.ds(0, 31)], plane_s.at[index])
    fine_store.wait()
    mid_store.wait()
    top_store.wait()


def body(
    fine_level,
    middle_level,
    coarse_level,
    two_input_weights,
    three_input_weights,
    depthwise,
    pointwise,
    bn_gain,
    bn_bias,
):
    devices = lax.axis_size(BATCH) * lax.axis_size("rows")
    counts = tuple(
        float(a.shape[0] * a.shape[1] * a.shape[2] * devices)
        for a in (fine_level, middle_level, coarse_level)
    )
    any_space = pl.BlockSpec(memory_space=pl.ANY)
    smem = pl.BlockSpec(memory_space=pltpu.SMEM)
    vmem = pltpu.VMEM
    dma = pltpu.SemaphoreType.DMA
    scratch = [
        vmem((10, 192, C), BF16),
        vmem((6, 96, C), BF16),
        vmem((4, 48, C), BF16),
        vmem((2, 4, 3, 3, C), BF16),
        vmem((2, 4, C, C), BF16),
        vmem((2, 4, C), F32),
        vmem((2, 4, C), F32),
        vmem((8, 9, 8, C), F32),
        vmem((192, 192), BF16),
        vmem((96, 96), BF16),
        vmem((192, 192), BF16),
        vmem((96, 96), BF16),
        vmem((10, 4, K, C), F32),
        vmem((10, 4, K, C), F32),
        vmem((6, 2, K, C), F32),
        vmem((6, 2, K, C), F32),
        vmem((6, 2, K, C), F32),
        vmem((4, K, C), F32),
        vmem((4, K, C), F32),
        vmem((4, 1, K, C), F32),
        vmem((6, 2, K, C), F32),
        vmem((4, 4, 2, K, C), F32),
        vmem((2, 8, 4, K, C), F32),
        vmem((2, 2, 1, K, C), F32),
        vmem((8, 2, K, C), F32),
        vmem((4, K, C), F32),
        vmem((6, 2, K, C), F32),
        vmem((4, K, C), F32),
        vmem((2 * 96, C), BF16),
        vmem((8, 5, 8, C), F32),
        vmem((2, 2, 2, K, C), BF16),
        vmem((2, 2, 2, K, C), BF16),
        vmem((2, 3, 2, K, C), BF16),
        vmem((2, 3, 2, K, C), BF16),
        vmem((2, 4, K, C), BF16),
        vmem((2, 4, K, C), BF16),
        vmem((2, 3, K, C), BF16),
        vmem((2, 3, K, C), BF16),
        vmem((2, 2, K, C), BF16),
        vmem((2, 2, K, C), BF16),
        vmem((2, K, C), BF16),
        vmem((2, K, C), BF16),
        vmem((8, 16, 8, 128), F32),
        vmem((8 * 16, 8, 128), F32),
        vmem((8, 192, C), BF16),
        vmem((4, 96, C), BF16),
        vmem((2, 48, C), BF16),
        dma((7,)),
        dma((3,)),
        dma((8,)),
        dma((8,)),
        dma((8,)),
        dma((8,)),
        dma((42,)),
        dma((42,)),
    ]
    return pl.pallas_call(
        functools.partial(kernel, counts),
        out_shape=tuple(
            jax.ShapeDtypeStruct(a.shape, BF16) for a in (fine_level, middle_level, coarse_level)
        ),
        in_specs=[any_space] * 3 + [smem] * 2 + [any_space] * 4,
        out_specs=(any_space,) * 3,
        scratch_shapes=scratch,
        name="bifpn",
        compiler_params=pltpu.CompilerParams(
            collective_id=0, has_side_effects=True, vmem_limit_bytes=60 * 1024 * 1024
        ),
    )(
        fine_level,
        middle_level,
        coarse_level,
        two_input_weights,
        three_input_weights,
        depthwise,
        pointwise,
        bn_gain,
        bn_bias,
    )


def solution(mesh):
    split = Mesh(
        mesh.devices.reshape(4, 4, 2, mesh.shape["rows"]), ("batch_0", "batch_1", "batch_2", "rows")
    )
    level = P(BATCH, "rows", None, None)
    return jax.shard_map(
        body,
        mesh=split,
        in_specs=(level,) * 3 + (P(),) * 6,
        out_specs=(level,) * 3,
        check_vma=False,
    )
```

time: 372 us -> 107 us (0.29)
  blocking collectives: 146 us -> 0 us
  Pallas kernels: 0 us -> 99.3 us
  waiting for transfers between devices: 68.5 us -> 0 us
  starting transfers between devices: 59.5 us -> 0 us
  other arithmetic: 47.8 us -> 0 us
  local copies, waits for them, and re-layouts: 26.8 us -> 6.64 us
  matrix products: 13.7 us -> 0 us
  between operations: 7.17 us -> 0.66 us
    all_to_all x11 -> x0, blocking collectives: 146 us -> none  [sent_to_all(): return lax.all_to_all(copies, axis, split_axis=0, concat_axis=0, tiled=True)]
    pallas_call x0 -> x1, Pallas kernels: none -> 99.3 us  [body(): pl.pallas_call(functools.partial(kernel, counts), out_shape=tuple((jax.Sh...]
    ppermute x20 -> x0, waiting for transfers between devices: 40.4 us -> none  [the longest x8 27.6 us: extended_2(): lax.ppermute(lax.slice_in_dim(block, 0, width, axis=dim), axis, backward)]
    ppermute x20 -> x0, starting transfers between devices: 38.8 us -> none  [the longest x8 22.9 us: extended_2(): lax.ppermute(lax.slice_in_dim(block, block.shape[dim] - width, None, axis...]
    convert_element_type x29 -> x0, other arithmetic: 29.2 us -> none  [the longest x8 17 us: weighted_join_activate(): return jax.nn.silu(running / weight_sum).astype(jnp.bfloat16)]
    all_to_all x5 -> x0, waiting for transfers between devices: 28.1 us -> none  [sent_to_all(): return lax.all_to_all(copies, axis, split_axis=0, concat_axis=0, tiled=True)]
    all_to_all x5 -> x0, starting transfers between devices: 20.8 us -> none  [sent_to_all(): return lax.all_to_all(copies, axis, split_axis=0, concat_axis=0, tiled=True)]
    dot_general x8 -> x0, matrix products: 13.7 us -> none  [separable(): jnp.dot(spatial.reshape(-1, spatial.shape[-1]), projection, preferred_ele...]
  transfers between devices with their start and end apart: 25 -> 0, of which waited for: 19 -> 0; matrix products, arithmetic and copies ran while one was open for 2% -> 0% of each run, Pallas kernels for 0% -> 0%
where the time goes in v1:
time: 107 us
  Pallas kernels  99.3 us (93%)
  local copies, waits for them, and re-layouts  6.64 us (6%)
    pallas_call x1, Pallas kernels, body(): pl.pallas_call(functools.partial(kernel, counts), out_shape=tuple((jax.Sh...  99.3 us
    unnamed x9, local copies, waits for them, and re-layouts  6.64 us

profile of v1, /device:TPU:1, one launch (start us, length us, event | category | flops | bytes accessed | tf_op | source)
XLA Modules:
  0.0 106.6 jit_solution(6764079360841930962)
XLA Ops:
  0.6 1.4 %copy.12.w2 = f32[2,3,2]{2,1,0:T(4,128)} copy(f32[2,3,2]{1,2,0:T(2,128)} %param.12) | data formatting | bytes 96 | tf_op args[3]
  2.0 1.5 %copy.13.dw_hbm = bf16[2,4,3,3,384]{4,3,2,1,0:T(4,128)(2,1)} copy(bf16[2,4,3,3,384]{4,1,3,2,0:T(4,128)(2,1)} %param.14) | data formatting | bytes 110592 | tf_op args[5]
  3.5 99.3 %bifpn.1 = (bf16[1,8,192,384]{3,2,1,0:T(8,128)(2,1)}, bf16[1,4,96,384]{3,2,1,0:T(8,128)(2,1)}, bf16[1,2,48,384]{3,2,1,0:T(8,128)(2,1)}) custom-call(bf16[1,8,192,384]{3,2,1,0:T(8,128)(2,1)} %fine_hbm.1, bf16[1,4,96,384]{3,2,1,0:T(8,128)(2,1)} %mid_hbm.1, bf16[1,2,48,384]{3,2,1,0:T(8,128)(2,1)} %top_hbm.1, f32[2,3,2]{2,1,0:T(4,128)} %copy.12.w2, f32[2,3]{1,0:T(2,128)} %w3.1, ...), custom_call_target="tpu_custom_call" | custom-call | tf_op jit(solution)/shard_map/bifpn/pallas_call | solution.py:802
  102.8 0.0 copy-start
  102.8 0.0 copy-start.1
  102.8 2.4 %copy.17 = bf16[1,8,192,384]{3,2,1,0:T(8,128)(2,1)} copy(bf16[1,8,192,384]{3,2,1,0:T(8,128)(2,1)} %get-tuple-element.6) | data formatting | bytes 2359296
  105.2 0.0 copy-done
  105.2 0.7 copy.18
  105.9 0.0 copy-done.1
  105.9 0.6 copy.19
Async XLA Ops:
  102.8 2.5 %copy-start = (bf16[1,4,96,384]{3,2,1,0:T(8,128)(2,1)S(1)}, bf16[1,4,96,384]{3,2,1,0:T(8,128)(2,1)}, u32[]{:S(2)}) copy-start(bf16[1,4,96,384]{3,2,1,0:T(8,128)(2,1)} %get-tuple-element.7) | copy-start | bytes 884740
  102.8 3.2 %copy-start.1 = (bf16[1,2,48,384]{3,2,1,0:T(8,128)(2,1)S(1)}, bf16[1,2,48,384]{3,2,1,0:T(8,128)(2,1)}, u32[]{:S(2)}) copy-start(bf16[1,2,48,384]{3,2,1,0:T(8,128)(2,1)} %get-tuple-element.8) | copy-start | bytes 221188

commit v2 on v1

--- a/solution.py
+++ b/solution.py
@@ -116,11 +116,7 @@
     send_c,
     ring,
     plane,
-    fine_res,
-    mid_res,
-    top_res,
     in_sem,
-    out_sem,
     ring_s,
     ring_r,
     plane_s,
@@ -130,8 +126,7 @@
 ):
     y, x = lax.axis_index("batch_0"), lax.axis_index("batch_1")
     core, z = lax.axis_index("batch_2"), lax.axis_index("rows")
-    in_ring = core * 8 + z
-    in_plane = y * 4 + x
+    in_plane = core * 16 + y * 4 + x
     is_hub = core == HUB
     has_above, has_below = z > 0, z < 7
 
@@ -159,7 +154,9 @@
         "mid": pltpu.make_async_copy(mid_hbm.at[0], mid_nat.at[pl.ds(1, 4)], in_sem.at[1]),
         "dw": pltpu.make_async_copy(dw_hbm, dw_in, in_sem.at[2]),
         "fine": pltpu.make_async_copy(fine_hbm.at[0], fine_nat.at[pl.ds(1, 8)], in_sem.at[3]),
-        "pw": pltpu.make_async_copy(pw_hbm, pw, in_sem.at[4]),
+        "pw": pltpu.make_async_copy(pw_hbm.at[0, 0], pw.at[0, 0], in_sem.at[4]),
+        "pw_0": pltpu.make_async_copy(pw_hbm.at[0, pl.ds(1, 3)], pw.at[0, pl.ds(1, 3)], in_sem.at[7]),
+        "pw_1": pltpu.make_async_copy(pw_hbm.at[1], pw.at[1], in_sem.at[8]),
         "gain": pltpu.make_async_copy(gain_hbm, gain, in_sem.at[5]),
         "bias": pltpu.make_async_copy(bias_hbm, bias, in_sem.at[6]),
     }
@@ -209,11 +206,11 @@
 
     loads["dw"].wait()
     for l in range(LAYERS):
-        for n in range(4):
-            for i in range(3):
-                taps = dw_in[l, n, i].astype(F32)
-                for j in range(3):
-                    dwb[l * 4 + n, 3 * i + j] = jnp.broadcast_to(taps[j : j + 1], (8, C))
+        for i in range(3):
+            for j in range(3):
+                taps = dw_in[l, i, j].astype(F32)
+                for n in range(4):
+                    dwb[l * 4 + n, 3 * i + j] = jnp.broadcast_to(taps[n : n + 1], (8, C))
 
     pl.semaphore_wait(barrier, 14 + 31)
 
@@ -282,116 +279,116 @@
         return [0.5 * one / acc for one in spread]
 
     def two(l, n):
-        return halves([w2[l, n, 0], w2[l, n, 1]])
+        return halves([w2[l, 0, n], w2[l, 1, n]])
 
     def three(l):
         return halves([w3[l, 0], w3[l, 1], w3[l, 2]])
 
-    def convolve(act, raw, index, height, planes, step_rows):
+    def convolve(act, raw, index, height, planes, step_rows, dot_rows):
         lanes = planes * K
+
+        def depthwise(r, at):
+            for c in range(3):
+                cs = pl.ds(c * 128, 128)
+                taps = [dwb[index, t, :, cs] for t in range(9)]
+                sums = []
+                for q in range(planes):
+                    rows = [tiles(act[r + i, q, :, cs]) for i in range(3)]
+                    sums.append(
+                        [
+                            flat(rows[0] * taps[j] + rows[1] * taps[3 + j] + rows[2] * taps[6 + j])
+                            for j in range(3)
+                        ]
+                    )
+                for q in range(planes):
+                    left = sums[q - 1][0] if q else shifted_down(sums[planes - 1][0])
+                    right = sums[q + 1][2] if q + 1 < planes else shifted_up(sums[0][2], 0.0)
+                    spat[pl.ds(at + q * K, K), cs] = (left + sums[q][1] + right).astype(BF16)
 
         def step(s, carry):
             total, squares = carry
-            for dr in range(step_rows):
-                r = s * step_rows + dr
-                for c in range(3):
-                    cs = pl.ds(c * 128, 128)
-                    taps = [dwb[index, t, :, cs] for t in range(9)]
-                    sums = []
+            for first in range(0, step_rows, dot_rows):
+                for dr in range(first, first + dot_rows):
+                    depthwise(s * step_rows + dr, dr * lanes)
+                out = jnp.dot(
+                    spat[pl.ds(first * lanes, dot_rows * lanes), :],
+                    pw[index // 4, index % 4],
+                    preferred_element_type=F32,
+                )
+                for dr in range(dot_rows):
                     for q in range(planes):
-                        rows = [tiles(act[r + i, q, :, cs]) for i in range(3)]
-                        sums.append(
-                            [
-                                flat(
-                                    rows[0] * taps[j] + rows[1] * taps[3 + j] + rows[2] * taps[6 + j]
-                                )
-                                for j in range(3)
-                            ]
-                        )
-                    for q in range(planes):
-                        left = sums[q - 1][0] if q else shifted_down(sums[planes - 1][0])
-                        right = sums[q + 1][2] if q + 1 < planes else shifted_up(sums[0][2], 0.0)
-                        spat[pl.ds(dr * lanes + q * K, K), cs] = (left + sums[q][1] + right).astype(
-                            BF16
-                        )
-            out = jnp.dot(
-                spat[pl.ds(0, step_rows * lanes), :],
-                pw[index // 4, index % 4],
-                preferred_element_type=F32,
-            )
-            for dr in range(step_rows):
-                for q in range(planes):
-                    at = dr * lanes + q * K
-                    raw[s * step_rows + dr, q] = out[at : at + K]
-            out = tiles(out)
-            return total + jnp.sum(out, axis=0), squares + jnp.sum(out * out, axis=0)
+                        at = dr * lanes + q * K
+                        raw[s * step_rows + first + dr, q] = out[at : at + K]
+                out = tiles(out)
+                total, squares = total + jnp.sum(out, axis=0), squares + jnp.sum(out * out, axis=0)
+            return total, squares
 
         start = (jnp.zeros((8, C), F32), jnp.zeros((8, C), F32))
         return lax.fori_loop(0, height // step_rows, step, start)
+
+    def slots(buffer, first, n):
+        return buffer.at[pl.ds(first, n), pl.ds(0, 6)]
+
+    def push(buffer, slot, sent, received, **device):
+        pltpu.make_async_remote_copy(
+            buffer.at[slot, pl.ds(0, 6)],
+            buffer.at[slot, pl.ds(0, 6)],
+            sent,
+            received,
+            device_id=device,
+            device_id_type=MESH_ID,
+        ).start()
+
+    def added(buffer, first, n):
+        terms = [buffer[first + k, 0:6] for k in range(n)]
+        while len(terms) > 1:
+            terms = [terms[k] + terms[k + 1] for k in range(0, len(terms), 2)]
+        return terms[0]
+
+    def plane_device(a, b):
+        return {"batch_0": lax.rem(y + a, 4), "batch_1": lax.rem(x + b, 4)}
 
     def reduce_start(index, stats, local_count):
         total, squares = stats
         total = jnp.sum(total, axis=0, keepdims=True)
         squares = jnp.sum(squares, axis=0, keepdims=True)
+        mine = index * 32 + in_plane
         for c in range(3):
-            ring[index, in_ring, c : c + 1, :] = total[:, c * 128 : (c + 1) * 128]
-            ring[index, in_ring, 3 + c : 4 + c, :] = squares[:, c * 128 : (c + 1) * 128]
+            plane[mine, c : c + 1, :] = total[:, c * 128 : (c + 1) * 128]
+            plane[mine, 3 + c : 4 + c, :] = squares[:, c * 128 : (c + 1) * 128]
         norm[index, 2] = jnp.broadcast_to(total * (1.0 / local_count), (8, C))
 
-        def to_hub(**device):
-            pltpu.make_async_remote_copy(
-                ring.at[index, in_ring],
-                ring.at[index, in_ring],
-                ring_s.at[index],
-                ring_r.at[index],
-                device_id=device,
-                device_id_type=MESH_ID,
-            ).start()
+        for a, b in XY_OFFSETS:
+            push(
+                plane, mine, plane_s.at[index], plane_r.at[index], **plane_device(a, b), batch_2=HUB
+            )
 
         @pl.when(jnp.logical_not(is_hub))
         def _():
-            for d in Z_OFFSETS + [0]:
-                to_hub(batch_2=HUB, rows=lax.rem(z + d, 8))
-
+            push(plane, mine, plane_s.at[index], plane_r.at[index], batch_2=HUB)
+
+    def reduce_middle(index):
         @pl.when(is_hub)
         def _():
+            wait_bytes(slots(plane, index * 32, 31), plane_r.at[index])
+            mine = index * 8 + z
+            ring[mine, 0:6] = added(plane, index * 32, 32)
             for d in Z_OFFSETS:
-                to_hub(rows=lax.rem(z + d, 8))
-            wait_bytes(ring.at[index, pl.ds(0, 15)], ring_r.at[index])
-            acc = ring[index, 0]
-            for k in range(1, 16):
-                acc = acc + ring[index, k]
-            plane[index * 16 + in_plane] = acc
-
-            def to_plane(**device):
-                pltpu.make_async_remote_copy(
-                    plane.at[index * 16 + in_plane],
-                    plane.at[index * 16 + in_plane],
-                    plane_s.at[index],
-                    plane_r.at[index],
-                    device_id=device,
-                    device_id_type=MESH_ID,
-                ).start()
-
-            for a, b in XY_OFFSETS:
-                at = {"batch_0": lax.rem(y + a, 4), "batch_1": lax.rem(x + b, 4)}
-                to_plane(**at, batch_2=1 - HUB)
-                to_plane(**at)
-            to_plane(batch_2=1 - HUB)
+                at = lax.rem(z + d, 8)
+                push(ring, mine, ring_s.at[index], ring_r.at[index], batch_2=1 - HUB, rows=at)
+                push(ring, mine, ring_s.at[index], ring_r.at[index], rows=at)
+            push(ring, mine, ring_s.at[index], ring_r.at[index], batch_2=1 - HUB)
 
     def reduce_end(index, count):
         @pl.when(is_hub)
         def _():
-            wait_bytes(plane.at[pl.ds(index * 16, 15)], plane_r.at[index])
+            wait_bytes(slots(ring, index * 8, 7), ring_r.at[index])
 
         @pl.when(jnp.logical_not(is_hub))
         def _():
-            wait_bytes(plane.at[pl.ds(index * 16, 16)], plane_r.at[index])
-
-        acc = plane[index * 16]
-        for k in range(1, 16):
-            acc = acc + plane[index * 16 + k]
-        acc = acc * (1.0 / count)
+            wait_bytes(slots(ring, index * 8, 8), ring_r.at[index])
+
+        acc = added(ring, index * 8, 8) * (1.0 / count)
         l, n = index // 4, index % 4
         for c in range(3):
             cs = pl.ds(c * 128, 128)
@@ -468,8 +465,6 @@
             for e in range(4):
                 top_in[e] = top_nat[e].astype(F32)
             loads["pw"].wait()
-            loads["gain"].wait()
-            loads["bias"].wait()
         else:
             scale, shift, shift_above, shift_below = scale_shift(3, None)
             for e in range(4):
@@ -487,7 +482,7 @@
 
         each(6, join_0)
         masked_edges(act_m, 5)
-        stats = convolve(act_m, mids, i0, 4, 2, 2)
+        stats = convolve(act_m, mids, i0, 4, 2, 4, 2)
         reduce_start(i0, stats, 4 * 96)
         for p in mid_pair:
             send_m[l, 0, p] = centred(mids[0, p], i0)
@@ -495,6 +490,7 @@
         up_0 = [(send_m.at[l, 0], halo_m.at[l, 1], 24 + 2 * l), mean_up(i0)]
         down_0 = [(send_m.at[l, 1], halo_m.at[l, 0], 25 + 2 * l), mean_down(i0)]
         send(up_0, down_0)
+        reduce_middle(i0)
 
         own, up = two(l, 1)
         if l == 0:
@@ -507,6 +503,7 @@
 
             each(10, place_fine)
         else:
+            receive(up_f, down_f)
             scale, shift, shift_above, shift_below = scale_shift(1, own)
 
             def place_fine(e):
@@ -519,6 +516,9 @@
                 base_f[9, q] = affine(halo_f[1, q], scale, shift_below)
 
         receive(up_0, down_0)
+        if l == 0:
+            for name in ("pw_0", "pw_1", "gain", "bias"):
+                loads[name].wait()
         reduce_end(i0, counts[1])
 
         scale, shift, shift_above, shift_below = scale_shift(i0, up)
@@ -541,7 +541,7 @@
 
         each(10, join_1)
         masked_edges(act_f, 9)
-        stats = convolve(act_f, fines, i1, 8, 4, 1)
+        stats = convolve(act_f, fines, i1, 8, 4, 4, 1)
         reduce_start(i1, stats, 8 * 192)
 
         def pool_columns(r):
@@ -558,13 +558,11 @@
         up_1 = [(send_p.at[l, pl.ds(0, 2)], halo_p.at[l, pl.ds(1, 2)], 28 + 2 * l), mean_up(i1)]
         down_1 = [(send_p.at[l, 2], halo_p.at[l, 0], 29 + 2 * l), mean_down(i1)]
         send(up_1, down_1)
+        reduce_middle(i1)
         if l == 0:
             for q in range(4):
                 send_f[0, q] = centred(fines[0, q], i1)
                 send_f[1, q] = centred(fines[7, q], i1)
-            up_f = [(send_f.at[0], halo_f.at[1], 32)]
-            down_f = [(send_f.at[1], halo_f.at[0], 33)]
-            send(up_f, down_f)
 
         w_mid, w_down, w_pool = three(l)
         scale, shift, shift_above, shift_below = scale_shift(i0, w_down)
@@ -609,7 +607,7 @@
 
         each(6, join_2)
         masked_edges(act_m, 5)
-        stats = convolve(act_m, nexts, i2, 4, 2, 2)
+        stats = convolve(act_m, nexts, i2, 4, 2, 4, 2)
         reduce_start(i2, stats, 4 * 96)
         for r in range(4):
             col_m[r] = column_pool(lambda q: nexts[r, q], 2)[0]
@@ -628,20 +626,18 @@
             up_t = [(send_t.at[0], halo_t.at[1], 38)]
             down_t = [(send_t.at[1], halo_t.at[0], 39)]
             send(up_t, down_t)
-            receive(up_f, down_f)
-        else:
+        reduce_middle(i2)
+        if l == 1:
             scale, shift, _, _ = scale_shift(i1, None)
 
             def finish_fine(r):
                 for q in range(4):
                     spat[pl.ds(q * K, K), :] = affine(fines[r, q], scale, shift).astype(BF16)
-                fine_res[r] = jnp.dot(
+                fine_out[0, r] = jnp.dot(
                     back_f[...], spat[pl.ds(0, 4 * K), :], preferred_element_type=F32
                 ).astype(BF16)
 
             each(8, finish_fine)
-            fine_store = pltpu.make_async_copy(fine_res, fine_out.at[0], out_sem.at[0])
-            fine_store.start()
         receive(up_2, down_2)
         mean_above, mean_below = norm[i2, 3], norm[i2, 4]
         pool_t[0] = jnp.maximum(flat(tiles(halo_q[l, 0].astype(F32)) + mean_above), col_m[0])
@@ -657,7 +653,7 @@
                 silu_of_double(tiles(base_t[e]) + (tiles(pool_t[e]) * scale + shift))
             )
         masked_edges(act_t, 3)
-        stats = convolve(act_t, tops, i3, 2, 1, 2)
+        stats = convolve(act_t, tops, i3, 2, 1, 2, 2)
         reduce_start(i3, stats, 2 * 48)
         scale, shift, shift_above, shift_below = scale_shift(i2, None)
         if l == 0:
@@ -666,6 +662,10 @@
             up_3 = [(send_c.at[0], halo_c.at[1], 40), mean_up(i3)]
             down_3 = [(send_c.at[1], halo_c.at[0], 41), mean_down(i3)]
             send(up_3, down_3)
+            up_f = [(send_f.at[0], halo_f.at[1], 32)]
+            down_f = [(send_f.at[1], halo_f.at[0], 33)]
+            send(up_f, down_f)
+            reduce_middle(i3)
             receive(up_t, down_t)
             for p in mid_pair:
                 mid_in[0, p] = affine(halo_t[0, p], scale, shift_above)
@@ -679,23 +679,20 @@
             receive(up_3, down_3)
             reduce_end(i3, counts[2])
         else:
+            reduce_middle(i3)
 
             def finish_mid(r):
                 for p in mid_pair:
                     spat[pl.ds(p * K, K), :] = affine(nexts[r, p], scale, shift).astype(BF16)
-                mid_res[r] = jnp.dot(
+                mid_out[0, r] = jnp.dot(
                     back_m[...], spat[pl.ds(0, 2 * K), :], preferred_element_type=F32
                 ).astype(BF16)
 
             each(4, finish_mid)
-            mid_store = pltpu.make_async_copy(mid_res, mid_out.at[0], out_sem.at[1])
-            mid_store.start()
             reduce_end(i3, counts[2])
             scale, shift, _, _ = scale_shift(i3, None)
             for e in range(2):
-                top_res[e] = affine(tops[e, 0], scale, shift).astype(BF16)
-            top_store = pltpu.make_async_copy(top_res, top_out.at[0], out_sem.at[2])
-            top_store.start()
+                top_out[0, e] = affine(tops[e, 0], scale, shift).astype(BF16)
 
     @pl.when(has_above)
     def _():
@@ -710,16 +707,24 @@
     @pl.when(jnp.logical_not(is_hub))
     def _():
         for index in range(8):
-            wait_bytes(ring.at[index, pl.ds(0, 8)], ring_s.at[index])
+            wait_bytes(slots(plane, 0, 16), plane_s.at[index])
 
     @pl.when(is_hub)
     def _():
         for index in range(8):
-            wait_bytes(ring.at[index, pl.ds(0, 7)], ring_s.at[index])
-            wait_bytes(plane.at[pl.ds(0, 31)], plane_s.at[index])
-    fine_store.wait()
-    mid_store.wait()
-    top_store.wait()
+            wait_bytes(slots(plane, 0, 15), plane_s.at[index])
+            wait_bytes(slots(ring, 0, 15), ring_s.at[index])
+
+
+def store_kernel(fine, mid, top, fine_out, mid_out, top_out, sems):
+    copies = [
+        pltpu.make_async_copy(src, dst, sems.at[i])
+        for i, (src, dst) in enumerate(((fine, fine_out), (mid, mid_out), (top, top_out)))
+    ]
+    for copy in copies:
+        copy.start()
+    for copy in copies:
+        copy.wait()
 
 
 def body(
@@ -746,7 +751,7 @@
         vmem((10, 192, C), BF16),
         vmem((6, 96, C), BF16),
         vmem((4, 48, C), BF16),
-        vmem((2, 4, 3, 3, C), BF16),
+        vmem((2, 3, 3, 4, C), BF16),
         vmem((2, 4, C, C), BF16),
         vmem((2, 4, C), F32),
         vmem((2, 4, C), F32),
@@ -771,7 +776,7 @@
         vmem((4, K, C), F32),
         vmem((6, 2, K, C), F32),
         vmem((4, K, C), F32),
-        vmem((2 * 96, C), BF16),
+        vmem((4 * 192, C), BF16),
         vmem((8, 5, 8, C), F32),
         vmem((2, 2, 2, K, C), BF16),
         vmem((2, 2, 2, K, C), BF16),
@@ -785,13 +790,9 @@
         vmem((2, 2, K, C), BF16),
         vmem((2, K, C), BF16),
         vmem((2, K, C), BF16),
-        vmem((8, 16, 8, 128), F32),
-        vmem((8 * 16, 8, 128), F32),
-        vmem((8, 192, C), BF16),
-        vmem((4, 96, C), BF16),
-        vmem((2, 48, C), BF16),
-        dma((7,)),
-        dma((3,)),
+        vmem((8 * 8, 8, 128), F32),
+        vmem((8 * 32, 8, 128), F32),
+        dma((9,)),
         dma((8,)),
         dma((8,)),
         dma((8,)),
@@ -799,13 +800,12 @@
         dma((42,)),
         dma((42,)),
     ]
-    return pl.pallas_call(
+    levels = (fine_level, middle_level, coarse_level)
+    results = pl.pallas_call(
         functools.partial(kernel, counts),
-        out_shape=tuple(
-            jax.ShapeDtypeStruct(a.shape, BF16) for a in (fine_level, middle_level, coarse_level)
-        ),
+        out_shape=tuple(vmem(a.shape, BF16) for a in levels),
         in_specs=[any_space] * 3 + [smem] * 2 + [any_space] * 4,
-        out_specs=(any_space,) * 3,
+        out_specs=(pl.BlockSpec(memory_space=vmem),) * 3,
         scratch_shapes=scratch,
         name="bifpn",
         compiler_params=pltpu.CompilerParams(
@@ -815,13 +815,21 @@
         fine_level,
         middle_level,
         coarse_level,
-        two_input_weights,
+        jnp.transpose(two_input_weights, (0, 2, 1)),
         three_input_weights,
-        depthwise,
+        jnp.transpose(depthwise, (0, 2, 3, 1, 4)),
         pointwise,
         bn_gain,
         bn_bias,
     )
+    return pl.pallas_call(
+        store_kernel,
+        out_shape=tuple(jax.ShapeDtypeStruct(a.shape, BF16) for a in levels),
+        in_specs=[pl.BlockSpec(memory_space=vmem)] * 3,
+        out_specs=(any_space,) * 3,
+        scratch_shapes=[dma((3,))],
+        name="store",
+    )(*(pltpu.with_memory_space_constraint(one, vmem) for one in results))
 
 
 def solution(mesh):

time: 107 us -> 97.4 us (0.910)
  local copies, waits for them, and re-layouts: 6.64 us -> 0 us
  Pallas kernels: 99.3 us -> 96.6 us
    unnamed x9 -> x0, local copies, waits for them, and re-layouts: 6.64 us -> none
    pallas_call x1 -> x2, Pallas kernels: 99.3 us -> 96.6 us  [the longest x1 95.5 us: body(): pl.pallas_call(functools.partial(kernel, counts), out_shape=tuple((vmem(a...]
where the time goes in v2:
time: 97.4 us; the launch traced here: 97.3 us
  Pallas kernels  96.6 us (99%)
    pallas_call x1, Pallas kernels, body(): pl.pallas_call(functools.partial(kernel, counts), out_shape=tuple((vmem(a...  95.5 us

profile of v2, /device:TPU:1, one launch (start us, length us, event | category | flops | bytes accessed | tf_op | source)
XLA Modules:
  0.0 97.3 jit_solution(4338339464119472223)
XLA Ops:
  0.6 95.5 %bifpn.1 = (bf16[1,8,192,384]{3,2,1,0:T(8,128)(2,1)S(1)}, bf16[1,4,96,384]{3,2,1,0:T(8,128)(2,1)S(1)}, bf16[1,2,48,384]{3,2,1,0:T(8,128)(2,1)S(1)}) custom-call(bf16[1,8,192,384]{3,2,1,0:T(8,128)(2,1)} %fine_hbm.1, bf16[1,4,96,384]{3,2,1,0:T(8,128)(2,1)} %mid_hbm.1, bf16[1,2,48,384]{3,2,1,0:T(8,128)(2,1)} %top_hbm.1, f32[2,2,3]{2,1,0:T(2,128)} %bitcast.3, ...), custom_call_target="tpu_custom_call" | custom-call | tf_op jit(solution)/shard_map/bifpn/pallas_call | solution.py:804
  96.1 1.1 %store.1 = (bf16[1,8,192,384]{3,2,1,0:T(8,128)(2,1)}, bf16[1,4,96,384]{3,2,1,0:T(8,128)(2,1)}, bf16[1,2,48,384]{3,2,1,0:T(8,128)(2,1)}) custom-call(bf16[1,8,192,384]{3,2,1,0:T(8,128)(2,1)S(1)} %get-tuple-element.6.fine, bf16[1,4,96,384]{3,2,1,0:T(8,128)(2,1)S(1)} %get-tuple-element.7.mid, bf16[1,2,48,384]{3,2,1,0:T(8,128)(2,1)S(1)} %get-tuple-element.8.top), custom_call_target="tpu_custom_call" | custom-call | tf_op jit(solution)/shard_map/store/pallas_call | solution.py:825

commit v3 on v2

--- a/solution.py
+++ b/solution.py
@@ -58,72 +58,80 @@
     pltpu.make_async_copy(ref, ref, sem).wait()
 
 
-def kernel(
-    counts,
-    fine_hbm,
-    mid_hbm,
-    top_hbm,
-    w2,
-    w3,
-    dw_hbm,
-    pw_hbm,
-    gain_hbm,
-    bias_hbm,
-    fine_out,
-    mid_out,
-    top_out,
-    fine_nat,
-    mid_nat,
-    top_nat,
-    dw_in,
-    pw,
-    gain,
-    bias,
-    dwb,
-    perm_f,
-    perm_m,
-    back_f,
-    back_m,
-    base_f,
-    act_f,
-    mid_in,
-    base_m,
-    act_m,
-    top_in,
-    base_t,
-    act_t,
-    lifted,
-    raw_m,
-    raw_f,
-    raw_t,
-    col_f,
-    col_m,
-    pool_m,
-    pool_t,
-    spat,
-    norm,
-    halo_m,
-    send_m,
-    halo_p,
-    send_p,
-    halo_f,
-    send_f,
-    halo_q,
-    send_q,
-    halo_t,
-    send_t,
-    halo_c,
-    send_c,
-    ring,
-    plane,
-    in_sem,
-    ring_s,
-    ring_r,
-    plane_s,
-    plane_r,
-    halo_s,
-    halo_r,
-):
+def kernel(counts, *refs):
+    pl.run_scoped(
+        functools.partial(layer_pair, counts, refs),
+        act_f=pltpu.VMEM((10, 4, K, C), BF16),
+        act_m=pltpu.VMEM((6, 2, K, C), BF16),
+        act_t=pltpu.VMEM((4, 1, K, C), BF16),
+        dwb=pltpu.VMEM((8, 9, 16, C), BF16),
+        spat=pltpu.VMEM((4 * 192, C), BF16),
+    )
+
+
+def layer_pair(counts, refs, act_f, act_m, act_t, dwb, spat):
+    (
+        fine_hbm,
+        mid_hbm,
+        top_hbm,
+        w2,
+        w3,
+        dw_hbm,
+        pw_hbm,
+        gain_hbm,
+        bias_hbm,
+        fine_out,
+        mid_out,
+        top_out,
+        fine_nat,
+        mid_nat,
+        top_nat,
+        dw_in,
+        pw,
+        gain,
+        bias,
+        perm_f,
+        perm_m,
+        back_f,
+        back_m,
+        base_f,
+        mid_in,
+        base_m,
+        top_in,
+        base_t,
+        lifted,
+        raw_m,
+        raw_f,
+        raw_t,
+        col_f,
+        col_m,
+        pool_m,
+        pool_t,
+        norm,
+        halo_m,
+        halo_a,
+        send_a,
+        send_m,
+        halo_p,
+        send_p,
+        halo_f,
+        send_f,
+        halo_q,
+        send_q,
+        halo_t,
+        send_t,
+        halo_c,
+        send_c,
+        ring,
+        plane,
+        in_sem,
+        ring_s,
+        ring_r,
+        plane_s,
+        plane_r,
+        halo_s,
+        halo_r,
+    ) = refs
     y, x = lax.axis_index("batch_0"), lax.axis_index("batch_1")
     core, z = lax.axis_index("batch_2"), lax.axis_index("rows")
     in_plane = core * 16 + y * 4 + x
@@ -185,7 +193,7 @@
         for l in range(LAYERS):
             for ref in (halo_m.at[l, 0], halo_p.at[l, 0], halo_q.at[l, 0]):
                 zeroed(ref)
-        for ref in (halo_f.at[0], halo_t.at[0], halo_c.at[0]):
+        for ref in (halo_f.at[0], halo_t.at[0], halo_c.at[0], halo_a.at[0]):
             zeroed(ref)
         for node in range(8):
             zeroed(norm.at[node, 3])
@@ -199,7 +207,7 @@
             for s in (1, 2):
                 for ref in (halo_p.at[l, s], halo_q.at[l, s]):
                     ref[...] = jnp.full(ref.shape, LOW, BF16)
-        for ref in (halo_f.at[1], halo_t.at[1], halo_c.at[1]):
+        for ref in (halo_f.at[1], halo_t.at[1], halo_c.at[1], halo_a.at[1]):
             zeroed(ref)
         for node in range(8):
             zeroed(norm.at[node, 4])
@@ -210,9 +218,7 @@
             for j in range(3):
                 taps = dw_in[l, i, j].astype(F32)
                 for n in range(4):
-                    dwb[l * 4 + n, 3 * i + j] = jnp.broadcast_to(taps[n : n + 1], (8, C))
-
-    pl.semaphore_wait(barrier, 14 + 31)
+                    dwb[l * 4 + n, 3 * i + j] = jnp.broadcast_to(taps[n : n + 1], (16, C)).astype(BF16)
 
     above = {"rows": jnp.maximum(z - 1, 0)}
     below = {"rows": jnp.minimum(z + 1, 7)}
@@ -253,22 +259,6 @@
         def _():
             for _, dst, slot in from_above:
                 wait_bytes(dst, halo_r.at[slot])
-
-    loads["top"].wait()
-    loads["mid"].wait()
-    first_up = [
-        (mid_nat.at[1], mid_nat.at[5], 0),
-        (top_nat.at[1], top_nat.at[3], 1),
-    ]
-    first_down = [
-        (mid_nat.at[4], mid_nat.at[0], 2),
-        (top_nat.at[2], top_nat.at[0], 3),
-    ]
-    send(first_up, first_down)
-    loads["fine"].wait()
-    fine_up = [(fine_nat.at[1], fine_nat.at[9], 4)]
-    fine_down = [(fine_nat.at[8], fine_nat.at[0], 5)]
-    send(fine_up, fine_down)
 
     def halves(weights):
         spread = [jnp.full((8, C), 1.0, F32) * w for w in weights]
@@ -284,8 +274,13 @@
     def three(l):
         return halves([w3[l, 0], w3[l, 1], w3[l, 2]])
 
-    def convolve(act, raw, index, height, planes, step_rows, dot_rows):
+    def convolve(
+        act, raw, index, height, planes, step_rows, dot_rows, order=None, before_rest=None
+    ):
         lanes = planes * K
+
+        def row_of(base, dr):
+            return base + dr if order is None else order[dr]
 
         def depthwise(r, at):
             for c in range(3):
@@ -293,23 +288,27 @@
                 taps = [dwb[index, t, :, cs] for t in range(9)]
                 sums = []
                 for q in range(planes):
-                    rows = [tiles(act[r + i, q, :, cs]) for i in range(3)]
+                    rows = [act[r + i, q, :, cs].reshape(K // 16, 16, 128) for i in range(3)]
                     sums.append(
                         [
                             flat(rows[0] * taps[j] + rows[1] * taps[3 + j] + rows[2] * taps[6 + j])
                             for j in range(3)
                         ]
                     )
+                left_edge = shifted_down(sums[planes - 1][0].astype(F32)).astype(BF16)
+                right_edge = shifted_up(sums[0][2].astype(F32), 0.0).astype(BF16)
                 for q in range(planes):
-                    left = sums[q - 1][0] if q else shifted_down(sums[planes - 1][0])
-                    right = sums[q + 1][2] if q + 1 < planes else shifted_up(sums[0][2], 0.0)
-                    spat[pl.ds(at + q * K, K), cs] = (left + sums[q][1] + right).astype(BF16)
+                    left = sums[q - 1][0] if q else left_edge
+                    right = sums[q + 1][2] if q + 1 < planes else right_edge
+                    spat[pl.ds(at + q * K, K), cs] = left + sums[q][1] + right
 
         def step(s, carry):
             total, squares = carry
             for first in range(0, step_rows, dot_rows):
+                if first and before_rest is not None:
+                    before_rest()
                 for dr in range(first, first + dot_rows):
-                    depthwise(s * step_rows + dr, dr * lanes)
+                    depthwise(row_of(s * step_rows, dr), dr * lanes)
                 out = jnp.dot(
                     spat[pl.ds(first * lanes, dot_rows * lanes), :],
                     pw[index // 4, index % 4],
@@ -318,7 +317,7 @@
                 for dr in range(dot_rows):
                     for q in range(planes):
                         at = dr * lanes + q * K
-                        raw[s * step_rows + first + dr, q] = out[at : at + K]
+                        raw[row_of(s * step_rows, first + dr), q] = out[at : at + K]
                 out = tiles(out)
                 total, squares = total + jnp.sum(out, axis=0), squares + jnp.sum(out * out, axis=0)
             return total, squares
@@ -453,18 +452,47 @@
         tops = raw_t.at[l]
 
         own, up = two(l, 0)
+
+        def join_0(e, act):
+            t = tiles(top_in[lax.div(e + 1, 2)]) * up
+            for p in mid_pair:
+                act[e, p] = flat(silu_of_double(tiles(mid_in[e, p]) * own + t)).astype(BF16)
+
         if l == 0:
-            receive(first_up, first_down)
 
             def place_mid(e):
                 out = jnp.dot(perm_m[...], mid_nat[e], preferred_element_type=F32)
                 for p in mid_pair:
                     mid_in[e, p] = out[p * K : (p + 1) * K]
 
-            each(6, place_mid)
-            for e in range(4):
+            loads["top"].wait()
+            loads["mid"].wait()
+            for e in (1, 2):
                 top_in[e] = top_nat[e].astype(F32)
+
+            def own_row(e):
+                place_mid(e + 1)
+                join_0(e + 1, act_m)
+
+            each(4, own_row)
+            send_a[0] = act_m[1]
+            send_a[1] = act_m[4]
+            pl.semaphore_wait(barrier, 14 + 31)
+            up_a = [(send_a.at[0], halo_a.at[1], 6)]
+            down_a = [(send_a.at[1], halo_a.at[0], 7)]
+            send(up_a, down_a)
+            loads["fine"].wait()
+            fine_up = [(fine_nat.at[1], fine_nat.at[9], 4)]
+            fine_down = [(fine_nat.at[8], fine_nat.at[0], 5)]
+            send(fine_up, fine_down)
             loads["pw"].wait()
+
+            def edge_rows():
+                receive(up_a, down_a)
+                act_m[0] = halo_a[0]
+                act_m[5] = halo_a[1]
+
+            stats = convolve(act_m, mids, i0, 4, 2, 4, 2, (1, 2, 0, 3), edge_rows)
         else:
             scale, shift, shift_above, shift_below = scale_shift(3, None)
             for e in range(4):
@@ -474,15 +502,9 @@
                     top_in[e] = affine(halo_c[1], scale, shift_below)
                 else:
                     top_in[e] = affine(raw_t[0, e - 1, 0], scale, shift)
-
-        def join_0(e):
-            t = tiles(top_in[lax.div(e + 1, 2)]) * up
-            for p in mid_pair:
-                act_m[e, p] = flat(silu_of_double(tiles(mid_in[e, p]) * own + t))
-
-        each(6, join_0)
-        masked_edges(act_m, 5)
-        stats = convolve(act_m, mids, i0, 4, 2, 4, 2)
+            each(6, lambda e: join_0(e, act_m))
+            masked_edges(act_m, 5)
+            stats = convolve(act_m, mids, i0, 4, 2, 4, 2)
         reduce_start(i0, stats, 4 * 96)
         for p in mid_pair:
             send_m[l, 0, p] = centred(mids[0, p], i0)
@@ -490,6 +512,16 @@
         up_0 = [(send_m.at[l, 0], halo_m.at[l, 1], 24 + 2 * l), mean_up(i0)]
         down_0 = [(send_m.at[l, 1], halo_m.at[l, 0], 25 + 2 * l), mean_down(i0)]
         send(up_0, down_0)
+        if l == 0:
+            first_up = [
+                (mid_nat.at[1], mid_nat.at[5], 0),
+                (top_nat.at[1], top_nat.at[3], 1),
+            ]
+            first_down = [
+                (mid_nat.at[4], mid_nat.at[0], 2),
+                (top_nat.at[2], top_nat.at[0], 3),
+            ]
+            send(first_up, first_down)
         reduce_middle(i0)
 
         own, up = two(l, 1)
@@ -502,6 +534,11 @@
                     base_f[e, q] = flat(tiles(out[q * K : (q + 1) * K]) * own)
 
             each(10, place_fine)
+            receive(first_up, first_down)
+            place_mid(0)
+            place_mid(5)
+            for e in (0, 3):
+                top_in[e] = top_nat[e].astype(F32)
         else:
             receive(up_f, down_f)
             scale, shift, shift_above, shift_below = scale_shift(1, own)
@@ -537,7 +574,7 @@
             for p in mid_pair:
                 t = lifted[m, p]
                 for q in (2 * p, 2 * p + 1):
-                    act_f[e, q] = silu_of_double(base_f[e, q] + t)
+                    act_f[e, q] = silu_of_double(base_f[e, q] + t).astype(BF16)
 
         each(10, join_1)
         masked_edges(act_f, 9)
@@ -603,7 +640,7 @@
             for p in mid_pair:
                 act_m[e, p] = flat(
                     silu_of_double(tiles(base_m[e, p]) + (tiles(pool_m[e, p]) * scale + shift))
-                )
+                ).astype(BF16)
 
         each(6, join_2)
         masked_edges(act_m, 5)
@@ -651,7 +688,7 @@
         for e in range(4):
             act_t[e, 0] = flat(
                 silu_of_double(tiles(base_t[e]) + (tiles(pool_t[e]) * scale + shift))
-            )
+            ).astype(BF16)
         masked_edges(act_t, 3)
         stats = convolve(act_t, tops, i3, 2, 1, 2, 2)
         reduce_start(i3, stats, 2 * 48)
@@ -755,19 +792,15 @@
         vmem((2, 4, C, C), BF16),
         vmem((2, 4, C), F32),
         vmem((2, 4, C), F32),
-        vmem((8, 9, 8, C), F32),
         vmem((192, 192), BF16),
         vmem((96, 96), BF16),
         vmem((192, 192), BF16),
         vmem((96, 96), BF16),
         vmem((10, 4, K, C), F32),
-        vmem((10, 4, K, C), F32),
-        vmem((6, 2, K, C), F32),
         vmem((6, 2, K, C), F32),
         vmem((6, 2, K, C), F32),
         vmem((4, K, C), F32),
         vmem((4, K, C), F32),
-        vmem((4, 1, K, C), F32),
         vmem((6, 2, K, C), F32),
         vmem((4, 4, 2, K, C), F32),
         vmem((2, 8, 4, K, C), F32),
@@ -776,9 +809,10 @@
         vmem((4, K, C), F32),
         vmem((6, 2, K, C), F32),
         vmem((4, K, C), F32),
-        vmem((4 * 192, C), BF16),
         vmem((8, 5, 8, C), F32),
         vmem((2, 2, 2, K, C), BF16),
+        vmem((2, 2, K, C), BF16),
+        vmem((2, 2, K, C), BF16),
         vmem((2, 2, 2, K, C), BF16),
         vmem((2, 3, 2, K, C), BF16),
         vmem((2, 3, 2, K, C), BF16),

time: 97.4 us -> 92.2 us (0.947)
  Pallas kernels: 96.6 us -> 91.4 us
    pallas_call x1, Pallas kernels: 95.5 us -> 90.3 us  [body(): pl.pallas_call(functools.partial(kernel, counts), out_shape=tuple((vmem(a...]
where the time goes in v3:
time: 92.2 us; the launch traced here: 92.1 us
  Pallas kernels  91.4 us (99%)
    pallas_call x1, Pallas kernels, body(): pl.pallas_call(functools.partial(kernel, counts), out_shape=tuple((vmem(a...  90.3 us

profile of v3, /device:TPU:1, one launch (start us, length us, event | category | flops | bytes accessed | tf_op | source)
XLA Modules:
  0.0 92.1 jit_solution(8755209373994819926)
XLA Ops:
  0.6 90.3 %bifpn.1 = (bf16[1,8,192,384]{3,2,1,0:T(8,128)(2,1)S(1)}, bf16[1,4,96,384]{3,2,1,0:T(8,128)(2,1)S(1)}, bf16[1,2,48,384]{3,2,1,0:T(8,128)(2,1)S(1)}) custom-call(bf16[1,8,192,384]{3,2,1,0:T(8,128)(2,1)} %refs_0_.1, bf16[1,4,96,384]{3,2,1,0:T(8,128)(2,1)} %refs_1_.1, bf16[1,2,48,384]{3,2,1,0:T(8,128)(2,1)} %refs_2_.1, f32[2,2,3]{2,1,0:T(2,128)} %bitcast.3, ...), custom_call_target="tpu_custom_call" | custom-call | tf_op jit(solution)/shard_map/bifpn/pallas_call | solution.py:838
  90.9 1.1 %store.1 = (bf16[1,8,192,384]{3,2,1,0:T(8,128)(2,1)}, bf16[1,4,96,384]{3,2,1,0:T(8,128)(2,1)}, bf16[1,2,48,384]{3,2,1,0:T(8,128)(2,1)}) custom-call(bf16[1,8,192,384]{3,2,1,0:T(8,128)(2,1)S(1)} %get-tuple-element.6.fine, bf16[1,4,96,384]{3,2,1,0:T(8,128)(2,1)S(1)} %get-tuple-element.7.mid, bf16[1,2,48,384]{3,2,1,0:T(8,128)(2,1)S(1)} %get-tuple-element.8.top), custom_call_target="tpu_custom_call" | custom-call | tf_op jit(solution)/shard_map/store/pallas_call | solution.py:859

commit v4 on v3

--- a/solution.py
+++ b/solution.py
@@ -131,6 +131,7 @@
         plane_r,
         halo_s,
         halo_r,
+        rounds,
     ) = refs
     y, x = lax.axis_index("batch_0"), lax.axis_index("batch_1")
     core, z = lax.axis_index("batch_2"), lax.axis_index("rows")
@@ -139,23 +140,34 @@
     has_above, has_below = z > 0, z < 7
 
     barrier = pltpu.get_barrier_semaphore()
-
-    def greet(**device):
-        pl.semaphore_signal(barrier, inc=1, device_id=device, device_id_type=MESH_ID)
-
-    for d in range(8):
-        for c in range(2):
-            if d:
-                greet(batch_2=lax.rem(core + c, 2), rows=lax.rem(z + d, 8))
-    for a in range(4):
-        for b in range(4):
-            for c in range(2):
-                if (a, b, c) != (0, 0, 0):
-                    greet(
-                        batch_0=lax.rem(y + a, 4),
-                        batch_1=lax.rem(x + b, 4),
-                        batch_2=lax.rem(core + c, 2),
-                    )
+    one_step = [
+        {axis: lax.rem(lax.axis_index(axis) + d, n)}
+        for axis, n in (("rows", 8), ("batch_0", 4), ("batch_1", 4))
+        for d in (1, n - 1)
+    ]
+
+    def greet(semaphore, devices):
+        for device in devices:
+            pl.semaphore_signal(semaphore, inc=1, device_id=device, device_id_type=MESH_ID)
+
+    greet(barrier, one_step + [{"batch_2": 1 - core}])
+
+    def entry_round(k):
+        if k:
+            pl.semaphore_wait(rounds.at[k - 1], 6)
+        else:
+            pl.semaphore_wait(barrier, 7)
+        if k < 3:
+            greet(rounds.at[k], one_step)
+
+    def entry_end():
+        @pl.when(is_hub)
+        def _():
+            greet(rounds.at[3], [{"batch_2": 1 - core}])
+
+        @pl.when(jnp.logical_not(is_hub))
+        def _():
+            pl.semaphore_wait(rounds.at[3], 1)
 
     loads = {
         "top": pltpu.make_async_copy(top_hbm.at[0], top_nat.at[pl.ds(1, 2)], in_sem.at[0]),
@@ -171,54 +183,16 @@
     for load in loads.values():
         load.start()
 
-    def permutation(ref, back, parts):
+    def zeroed(ref):
+        ref[...] = jnp.zeros(ref.shape, ref.dtype)
+
+    def permutation(ref, parts, inverse):
         n = parts * K
         row = lax.broadcasted_iota(jnp.int32, (n, n), 0)
         col = lax.broadcasted_iota(jnp.int32, (n, n), 1)
+        if inverse:
+            row, col = col, row
         ref[...] = jnp.where(lax.rem(row, K) * parts + lax.div(row, K) == col, 1.0, 0.0).astype(BF16)
-        back[...] = jnp.where(lax.rem(col, K) * parts + lax.div(col, K) == row, 1.0, 0.0).astype(
-            BF16
-        )
-
-    permutation(perm_m, back_m, 2)
-    permutation(perm_f, back_f, 4)
-
-    def zeroed(ref):
-        ref[...] = jnp.zeros(ref.shape, ref.dtype)
-
-    @pl.when(z == 0)
-    def _():
-        for ref in (fine_nat.at[0], mid_nat.at[0], top_nat.at[0]):
-            zeroed(ref)
-        for l in range(LAYERS):
-            for ref in (halo_m.at[l, 0], halo_p.at[l, 0], halo_q.at[l, 0]):
-                zeroed(ref)
-        for ref in (halo_f.at[0], halo_t.at[0], halo_c.at[0], halo_a.at[0]):
-            zeroed(ref)
-        for node in range(8):
-            zeroed(norm.at[node, 3])
-
-    @pl.when(z == 7)
-    def _():
-        for ref in (fine_nat.at[9], mid_nat.at[5], top_nat.at[3]):
-            zeroed(ref)
-        for l in range(LAYERS):
-            zeroed(halo_m.at[l, 1])
-            for s in (1, 2):
-                for ref in (halo_p.at[l, s], halo_q.at[l, s]):
-                    ref[...] = jnp.full(ref.shape, LOW, BF16)
-        for ref in (halo_f.at[1], halo_t.at[1], halo_c.at[1], halo_a.at[1]):
-            zeroed(ref)
-        for node in range(8):
-            zeroed(norm.at[node, 4])
-
-    loads["dw"].wait()
-    for l in range(LAYERS):
-        for i in range(3):
-            for j in range(3):
-                taps = dw_in[l, i, j].astype(F32)
-                for n in range(4):
-                    dwb[l * 4 + n, 3 * i + j] = jnp.broadcast_to(taps[n : n + 1], (16, C)).astype(BF16)
 
     above = {"rows": jnp.maximum(z - 1, 0)}
     below = {"rows": jnp.minimum(z + 1, 7)}
@@ -273,6 +247,42 @@
 
     def three(l):
         return halves([w3[l, 0], w3[l, 1], w3[l, 2]])
+
+    def spread_taps():
+        loads["dw"].wait()
+        for l in range(LAYERS):
+            for i in range(3):
+                for j in range(3):
+                    taps = dw_in[l, i, j].astype(F32)
+                    for n in range(4):
+                        dwb[l * 4 + n, 3 * i + j] = jnp.broadcast_to(taps[n : n + 1], (16, C)).astype(BF16)
+
+    def fill_edges():
+        @pl.when(z == 0)
+        def _():
+            for ref in (fine_nat.at[0], mid_nat.at[0], top_nat.at[0]):
+                zeroed(ref)
+            for l in range(LAYERS):
+                for ref in (halo_m.at[l, 0], halo_p.at[l, 0], halo_q.at[l, 0]):
+                    zeroed(ref)
+            for ref in (halo_f.at[0], halo_t.at[0], halo_c.at[0], halo_a.at[0]):
+                zeroed(ref)
+            for node in range(8):
+                zeroed(norm.at[node, 3])
+
+        @pl.when(z == 7)
+        def _():
+            for ref in (fine_nat.at[9], mid_nat.at[5], top_nat.at[3]):
+                zeroed(ref)
+            for l in range(LAYERS):
+                zeroed(halo_m.at[l, 1])
+                for s in (1, 2):
+                    for ref in (halo_p.at[l, s], halo_q.at[l, s]):
+                        ref[...] = jnp.full(ref.shape, LOW, BF16)
+            for ref in (halo_f.at[1], halo_t.at[1], halo_c.at[1], halo_a.at[1]):
+                zeroed(ref)
+            for node in range(8):
+                zeroed(norm.at[node, 4])
 
     def convolve(
         act, raw, index, height, planes, step_rows, dot_rows, order=None, before_rest=None
@@ -427,12 +437,13 @@
         def _():
             zeroed(act.at[last])
 
-    def each(n, fn):
+    def each(n, fn, at_once=1):
         def step(i, _):
-            fn(i)
+            for k in range(at_once):
+                fn(i * at_once + k)
             return 0
 
-        lax.fori_loop(0, n, step, 0)
+        lax.fori_loop(0, n // at_once, step, 0)
 
     def column_pool(load, planes):
         out = []
@@ -465,22 +476,25 @@
                 for p in mid_pair:
                     mid_in[e, p] = out[p * K : (p + 1) * K]
 
+            permutation(perm_m, 2, False)
             loads["top"].wait()
             loads["mid"].wait()
             for e in (1, 2):
                 top_in[e] = top_nat[e].astype(F32)
-
-            def own_row(e):
-                place_mid(e + 1)
-                join_0(e + 1, act_m)
-
-            each(4, own_row)
+            for e in (1, 4):
+                place_mid(e)
+                join_0(e, act_m)
             send_a[0] = act_m[1]
             send_a[1] = act_m[4]
-            pl.semaphore_wait(barrier, 14 + 31)
+            entry_round(0)
             up_a = [(send_a.at[0], halo_a.at[1], 6)]
             down_a = [(send_a.at[1], halo_a.at[0], 7)]
             send(up_a, down_a)
+            for e in (2, 3):
+                place_mid(e)
+                join_0(e, act_m)
+            fill_edges()
+            spread_taps()
             loads["fine"].wait()
             fine_up = [(fine_nat.at[1], fine_nat.at[9], 4)]
             fine_down = [(fine_nat.at[8], fine_nat.at[0], 5)]
@@ -488,6 +502,10 @@
             loads["pw"].wait()
 
             def edge_rows():
+                permutation(perm_f, 4, False)
+                for k in (1, 2, 3):
+                    entry_round(k)
+                entry_end()
                 receive(up_a, down_a)
                 act_m[0] = halo_a[0]
                 act_m[5] = halo_a[1]
@@ -502,7 +520,7 @@
                     top_in[e] = affine(halo_c[1], scale, shift_below)
                 else:
                     top_in[e] = affine(raw_t[0, e - 1, 0], scale, shift)
-            each(6, lambda e: join_0(e, act_m))
+            each(6, lambda e: join_0(e, act_m), 3)
             masked_edges(act_m, 5)
             stats = convolve(act_m, mids, i0, 4, 2, 4, 2)
         reduce_start(i0, stats, 4 * 96)
@@ -567,7 +585,7 @@
             for p in mid_pair:
                 lifted[e + 1, p] = affine(mids[e, p], scale, shift)
 
-        each(4, lift)
+        each(4, lift, 2)
 
         def join_1(e):
             m = lax.div(e + 1, 2)
@@ -576,9 +594,9 @@
                 for q in (2 * p, 2 * p + 1):
                     act_f[e, q] = silu_of_double(base_f[e, q] + t).astype(BF16)
 
-        each(10, join_1)
+        each(10, join_1, 2)
         masked_edges(act_f, 9)
-        stats = convolve(act_f, fines, i1, 8, 4, 4, 1)
+        stats = convolve(act_f, fines, i1, 8, 4, 4, 2)
         reduce_start(i1, stats, 8 * 192)
 
         def pool_columns(r):
@@ -642,7 +660,7 @@
                     silu_of_double(tiles(base_m[e, p]) + (tiles(pool_m[e, p]) * scale + shift))
                 ).astype(BF16)
 
-        each(6, join_2)
+        each(6, join_2, 3)
         masked_edges(act_m, 5)
         stats = convolve(act_m, nexts, i2, 4, 2, 4, 2)
         reduce_start(i2, stats, 4 * 96)
@@ -666,6 +684,9 @@
         reduce_middle(i2)
         if l == 1:
             scale, shift, _, _ = scale_shift(i1, None)
+
+            permutation(back_f, 4, True)
+            permutation(back_m, 2, True)
 
             def finish_fine(r):
                 for q in range(4):
@@ -833,6 +854,7 @@
         dma((8,)),
         dma((42,)),
         dma((42,)),
+        pltpu.SemaphoreType.REGULAR((4,)),
     ]
     levels = (fine_level, middle_level, coarse_level)
     results = pl.pallas_call(

time: 92.2 us -> 90.7 us (0.984)
  Pallas kernels: 91.4 us -> 89.9 us
    pallas_call x1, Pallas kernels: 90.3 us -> 88.8 us  [body(): pl.pallas_call(functools.partial(kernel, counts), out_shape=tuple((vmem(a...]
where the time goes in v4:
time: 90.7 us; the launch traced here: 90.6 us
  Pallas kernels  89.9 us (99%)
    pallas_call x1, Pallas kernels, body(): pl.pallas_call(functools.partial(kernel, counts), out_shape=tuple((vmem(a...  88.8 us

profile of v4, /device:TPU:1, one launch (start us, length us, event | category | flops | bytes accessed | tf_op | source)
XLA Modules:
  0.0 90.6 jit_solution(11206698464949333486)
XLA Ops:
  0.6 88.8 %bifpn.1 = (bf16[1,8,192,384]{3,2,1,0:T(8,128)(2,1)S(1)}, bf16[1,4,96,384]{3,2,1,0:T(8,128)(2,1)S(1)}, bf16[1,2,48,384]{3,2,1,0:T(8,128)(2,1)S(1)}) custom-call(bf16[1,8,192,384]{3,2,1,0:T(8,128)(2,1)} %refs_0_.1, bf16[1,4,96,384]{3,2,1,0:T(8,128)(2,1)} %refs_1_.1, bf16[1,2,48,384]{3,2,1,0:T(8,128)(2,1)} %refs_2_.1, f32[2,2,3]{2,1,0:T(2,128)} %bitcast.3, ...), custom_call_target="tpu_custom_call" | custom-call | tf_op jit(solution)/shard_map/bifpn/pallas_call | solution.py:860
  89.4 1.1 %store.1 = (bf16[1,8,192,384]{3,2,1,0:T(8,128)(2,1)}, bf16[1,4,96,384]{3,2,1,0:T(8,128)(2,1)}, bf16[1,2,48,384]{3,2,1,0:T(8,128)(2,1)}) custom-call(bf16[1,8,192,384]{3,2,1,0:T(8,128)(2,1)S(1)} %get-tuple-element.6.fine, bf16[1,4,96,384]{3,2,1,0:T(8,128)(2,1)S(1)} %get-tuple-element.7.mid, bf16[1,2,48,384]{3,2,1,0:T(8,128)(2,1)S(1)} %get-tuple-element.8.top), custom_call_target="tpu_custom_call" | custom-call | tf_op jit(solution)/shard_map/store/pallas_call | solution.py:881

commit v5 on v4

--- a/solution.py
+++ b/solution.py
@@ -65,7 +65,7 @@
         act_m=pltpu.VMEM((6, 2, K, C), BF16),
         act_t=pltpu.VMEM((4, 1, K, C), BF16),
         dwb=pltpu.VMEM((8, 9, 16, C), BF16),
-        spat=pltpu.VMEM((4 * 192, C), BF16),
+        spat=pltpu.VMEM((8 * 192, C), BF16),
     )
 
 
@@ -209,7 +209,7 @@
 
     sends_up, sends_down = [], []
 
-    def send(up, down):
+    def start_sends(up, down):
         @pl.when(has_above)
         def _():
             for one in up:
@@ -220,6 +220,8 @@
             for one in down:
                 to_below(*one).start()
 
+    def send(up, down):
+        start_sends(up, down)
         sends_up.extend(up)
         sends_down.extend(down)
 
@@ -402,7 +404,7 @@
         for c in range(3):
             cs = pl.ds(c * 128, 128)
             center = acc[c : c + 1]
-            spread = acc[3 + c : 4 + c] - center * center
+            spread = jnp.maximum(acc[3 + c : 4 + c] - center * center, 0.0)
             scale = gain[l, n : n + 1, cs] * lax.rsqrt(spread + EPS)
             shift = bias[l, n : n + 1, cs] - center * scale
             norm[index, 0, :, cs] = jnp.broadcast_to(scale, (8, 128))
@@ -489,11 +491,23 @@
             entry_round(0)
             up_a = [(send_a.at[0], halo_a.at[1], 6)]
             down_a = [(send_a.at[1], halo_a.at[0], 7)]
-            send(up_a, down_a)
+
+            @pl.when(jnp.logical_not(is_hub))
+            def _():
+                start_sends(up_a, down_a)
+
             for e in (2, 3):
                 place_mid(e)
                 join_0(e, act_m)
+
+            @pl.when(is_hub)
+            def _():
+                start_sends(up_a, down_a)
+
+            sends_up.extend(up_a)
+            sends_down.extend(down_a)
             fill_edges()
+            entry_round(1)
             spread_taps()
             loads["fine"].wait()
             fine_up = [(fine_nat.at[1], fine_nat.at[9], 4)]
@@ -503,14 +517,14 @@
 
             def edge_rows():
                 permutation(perm_f, 4, False)
-                for k in (1, 2, 3):
-                    entry_round(k)
-                entry_end()
+                entry_round(2)
                 receive(up_a, down_a)
                 act_m[0] = halo_a[0]
                 act_m[5] = halo_a[1]
 
             stats = convolve(act_m, mids, i0, 4, 2, 4, 2, (1, 2, 0, 3), edge_rows)
+            entry_round(3)
+            entry_end()
         else:
             scale, shift, shift_above, shift_below = scale_shift(3, None)
             for e in range(4):
@@ -596,7 +610,7 @@
 
         each(10, join_1, 2)
         masked_edges(act_f, 9)
-        stats = convolve(act_f, fines, i1, 8, 4, 4, 2)
+        stats = convolve(act_f, fines, i1, 8, 4, 8, 2)
         reduce_start(i1, stats, 8 * 192)
 
         def pool_columns(r):

time: 90.7 us -> 90.2 us (level)
  no operation moved by 1% of the time
where the time goes in v5:
time: 90.2 us; the launch traced here: 90.1 us
  Pallas kernels  89.4 us (99%)
    pallas_call x1, Pallas kernels, body(): pl.pallas_call(functools.partial(kernel, counts), out_shape=tuple((vmem(a...  88.3 us

profile of v5, /device:TPU:1, one launch (start us, length us, event | category | flops | bytes accessed | tf_op | source)
XLA Modules:
  0.0 90.1 jit_solution(3049283186683450443)
XLA Ops:
  0.6 88.3 %bifpn.1 = (bf16[1,8,192,384]{3,2,1,0:T(8,128)(2,1)S(1)}, bf16[1,4,96,384]{3,2,1,0:T(8,128)(2,1)S(1)}, bf16[1,2,48,384]{3,2,1,0:T(8,128)(2,1)S(1)}) custom-call(bf16[1,8,192,384]{3,2,1,0:T(8,128)(2,1)} %refs_0_.1, bf16[1,4,96,384]{3,2,1,0:T(8,128)(2,1)} %refs_1_.1, bf16[1,2,48,384]{3,2,1,0:T(8,128)(2,1)} %refs_2_.1, f32[2,2,3]{2,1,0:T(2,128)} %bitcast.3, ...), custom_call_target="tpu_custom_call" | custom-call | tf_op jit(solution)/shard_map/bifpn/pallas_call | solution.py:874
  88.9 1.1 %store.1 = (bf16[1,8,192,384]{3,2,1,0:T(8,128)(2,1)}, bf16[1,4,96,384]{3,2,1,0:T(8,128)(2,1)}, bf16[1,2,48,384]{3,2,1,0:T(8,128)(2,1)}) custom-call(bf16[1,8,192,384]{3,2,1,0:T(8,128)(2,1)S(1)} %get-tuple-element.6.fine, bf16[1,4,96,384]{3,2,1,0:T(8,128)(2,1)S(1)} %get-tuple-element.7.mid, bf16[1,2,48,384]{3,2,1,0:T(8,128)(2,1)S(1)} %get-tuple-element.8.top), custom_call_target="tpu_custom_call" | custom-call | tf_op jit(solution)/shard_map/store/pallas_call | solution.py:895
